TPU v7x, 32 devices: a whole 2x2x4 slice. The times are simulated.
32 devices in a mesh: section: 2 (over x), dp: 4 (over z), tensor: 4 (over y, core).
Axes of the slice: x: 2, y: 2, z: 4, core: 2. Of those that a mesh axis runs over, the one named last changes fastest.
Arguments:
- images: bfloat16 [4, 4, 577, 1024], P(None, 'dp', None, 'tensor'), may hold values from -6 to 6
- cotangent: bfloat16 [4, 4, 577, 1024], P(None, 'dp', None, 'tensor'), may hold values from -6 to 6
- ln1_gain: float32 [2, 1024], P('section', 'tensor'), may hold values from 0.5 to 1.5
- ln1_bias: float32 [2, 1024], P('section', 'tensor'), may hold values from -1.8 to 1.8
- qkv_weight: bfloat16 [2, 3, 1024, 1024], P('section', None, None, 'tensor'), may hold values from -6.25 to 6.25
- qv_bias: float32 [2, 2, 1024], P('section', None, 'tensor'), may hold values from -3 to 3
- out_weight: bfloat16 [2, 1024, 1024], P('section', 'tensor'), may hold values from -1 to 1
- out_bias: float32 [2, 1024], P('section', 'tensor'), may hold values from -3 to 3
- ln2_gain: float32 [2, 1024], P('section', 'tensor'), may hold values from 0.5 to 1.5
- ln2_bias: float32 [2, 1024], P('section', 'tensor'), may hold values from -1.8 to 1.8
- fc1_weight: bfloat16 [2, 1024, 4096], P('section', None, 'tensor'), may hold values from -0.1875 to 0.1875
- fc1_bias: float32 [2, 4096], P('section', 'tensor'), may hold values from -3 to 3
- fc2_weight: bfloat16 [2, 4096, 1024], P('section', 'tensor'), may hold values from -0.09375 to 0.09375
- fc2_bias: float32 [2, 1024], P('section', 'tensor'), may hold values from -3 to 3
Outputs:
- section_out: bfloat16 [2, 4, 4, 577, 1024], P('section', None, 'dp', None, 'tensor')
- input_grads: float32 [2, 4, 4, 577, 1024], P('section', None, 'dp', None, 'tensor')
- grad_ln1_gain: float32 [2, 1024], P('section', 'tensor')
- grad_ln1_bias: float32 [2, 1024], P('section', 'tensor')
- grad_qkv_weight: float32 [2, 3, 1024, 1024], P('section', None, None, 'tensor')
- grad_qv_bias: float32 [2, 2, 1024], P('section', None, 'tensor')
- grad_out_weight: float32 [2, 1024, 1024], P('section', 'tensor')
- grad_out_bias: float32 [2, 1024], P('section', 'tensor')
- grad_ln2_gain: float32 [2, 1024], P('section', 'tensor')
- grad_ln2_bias: float32 [2, 1024], P('section', 'tensor')
- grad_fc1_weight: float32 [2, 1024, 4096], P('section', None, 'tensor')
- grad_fc1_bias: float32 [2, 4096], P('section', 'tensor')
- grad_fc2_weight: float32 [2, 4096, 1024], P('section', 'tensor')
- grad_fc2_bias: float32 [2, 1024], P('section', 'tensor')
All inputs are finite; a program needn't handle non-finite values.
Results may differ from a plain program's by a relative error of at most 0.02.
The roundings to bfloat16 on the way count: a program that leaves them out, or rounds other values in their place, can miss the bound.
Values may be sent and summed in bfloat16 or wider, within the bound.
A program may use at most 320 MiB of HBM per device.

v0:
```python
import functools
import types

import jax
import jax.numpy as jnp
from jax import lax
from jax.experimental import pallas as pl
from jax.experimental.pallas import tpu as pltpu
from jax.sharding import PartitionSpec as P

BF16, F32 = jnp.bfloat16, jnp.float32
HEAD_DIM = 64
EPSILON = 1e-06
ROOT_HALF = 0.7071067811865476
GAUSS_FACTOR = 0.3989422804014327
MASKED = -1e30
STEP = 32
ANY = pl.BlockSpec(memory_space=pl.ANY)
VMEM_BYTES = 67043328

LN1_GAIN, LN1_BIAS, Q_BIAS, V_BIAS, OUT_BIAS, LN2_GAIN, LN2_BIAS, FC2_BIAS, FC1_BIAS = range(9)
VECTOR_ROWS = 16


def flip(place, bit):
    return place + bit - 2 * bit * lax.rem(lax.div(place, bit), 2)


def partner(place, slot):
    bit = 1
    while bit <= slot:
        if slot & bit:
            place = flip(place, bit)
        bit *= 2
    return place


def sizes_of(images, fc1_weight, tensor):
    micro, _, tok, width = images.shape
    dm = types.SimpleNamespace()
    dm.T, dm.W, dm.micro, dm.tok = tensor, width, micro, tok
    dm.D = width * tensor
    dm.FL = fc1_weight.shape[2]
    dm.RP = -(-tok // STEP) * STEP
    dm.RL = -(-tok // 128) * 128
    dm.C = min(512, dm.FL)
    dm.NC = dm.FL // dm.C
    dm.order = [
        (2 * p + half, c) for p in range(tensor // 2) for c in range(dm.NC) for half in range(2)
    ]
    dm.NI = len(dm.order)
    dm.NCH = 2 + 2 * dm.NC
    return dm


def full_vector(dm, vectors, row):
    return jnp.concatenate([vectors[j, row : row + 1, :] for j in range(dm.T)], axis=1)


def norm_rows(rows, width):
    mean = jnp.sum(rows, axis=1, keepdims=True) * (1.0 / width)
    var = jnp.sum(rows * rows, axis=1, keepdims=True) * (1.0 / width) - mean * mean
    inv = lax.rsqrt(var + EPSILON)
    return (rows - mean) * inv, inv


def block_rows(dm, ref, rows):
    return jnp.concatenate([ref[j, rows, :] for j in range(dm.T)], axis=1)


def dot_last(left, right):
    return lax.dot_general(left, right, (((1,), (1,)), ((), ())), preferred_element_type=F32)


def dot_plain(left, right):
    return lax.dot_general(left, right, (((1,), (0,)), ((), ())), preferred_element_type=F32)


def half_masks(rows):
    lane = lax.broadcasted_iota(jnp.int32, (rows, 128), 1)
    return [lane < HEAD_DIM, lane >= HEAD_DIM]


def chunk_refs(dm, index, qkv, out, up, down):
    if index == 0:
        return qkv
    if index == 1:
        return out
    c = (index - 2) // 2
    if index % 2 == 0:
        return up.at[:, pl.ds(c * dm.C, dm.C)]
    return down.at[pl.ds(c * dm.C, dm.C), :]


def meet(dm, section, tensor):
    barrier = pltpu.get_barrier_semaphore()
    for slot in range(1, dm.T):
        pl.semaphore_signal(barrier, inc=1, device_id={"tensor": partner(tensor, slot)})
    pl.semaphore_signal(barrier, inc=1, device_id={"section": 1 - section})
    pl.semaphore_wait(barrier, dm.T)


def forward_kernel(
    dm,
    xin, spin, wqkv, wout, wup, wdown,
    gqkv, gout, gup, gdown, xc, xkeep, qkeep, kkeep, vkeep, okeep, hkeep, akeep, spkeep, result,
    xarr, n1, wq, wob, w1b, w2b, ab, gb, acc, n2, yb, b1r, spb, q, k, v, o,
    wsend, wrecv, xsend, xrecv, psend, precv, osend, orecv, ssem, lsem, lw, la,
):
    section, tensor = lax.axis_index("section"), lax.axis_index("tensor")
    T, W, D, RP, RL, C, NI = dm.T, dm.W, dm.D, dm.RP, dm.RL, dm.C, dm.NI
    lower, upper = section == 0, section == 1
    own = (wqkv, wout, wup, wdown)

    def slot_refs(slot):
        return (gqkv.at[slot], gout.at[slot], gup.at[slot], gdown.at[slot])

    def weight_copy(slot, index):
        relay = slot > 1 and slot % 2 == 1
        source = chunk_refs(dm, index, *(slot_refs(slot - 1) if relay else own))
        return pltpu.make_async_remote_copy(
            src_ref=source,
            dst_ref=chunk_refs(dm, index, *slot_refs(slot)),
            send_sem=wsend.at[slot, index],
            recv_sem=wrecv.at[slot, index],
            device_id={"tensor": flip(tensor, 1) if relay else partner(tensor, slot)},
        )

    def input_copy(slot):
        return pltpu.make_async_remote_copy(
            src_ref=xin.at[lax.rem(partner(tensor, slot), dm.micro)],
            dst_ref=xc.at[tensor],
            send_sem=xsend.at[slot],
            recv_sem=xrecv.at[slot],
            device_id={"tensor": partner(tensor, slot)},
        )

    def vector_copy(slot):
        return pltpu.make_async_remote_copy(
            src_ref=spin,
            dst_ref=spb.at[tensor],
            send_sem=psend.at[slot],
            recv_sem=precv.at[slot],
            device_id={"tensor": partner(tensor, slot)},
        )

    def output_copy(slot):
        return pltpu.make_async_remote_copy(
            src_ref=yb.at[partner(tensor, slot)],
            dst_ref=result.at[tensor],
            send_sem=osend.at[slot],
            recv_sem=orecv.at[slot],
            device_id={"tensor": partner(tensor, slot)},
        )

    stream_copy = pltpu.make_async_remote_copy(
        src_ref=yb,
        dst_ref=xarr,
        send_sem=ssem.at[0],
        recv_sem=ssem.at[1],
        device_id={"section": 1 - section},
    )

    meet(dm, section, tensor)
    for slot in range(1, T):
        vector_copy(slot).start()
        input_copy(slot).start()
    own_vec = pltpu.make_async_copy(spin, spb.at[tensor], lsem.at[0])
    own_vec.start()
    own_in = pltpu.make_async_copy(xin.at[lax.rem(tensor, dm.micro)], xc.at[tensor], lsem.at[1])
    own_in.start()
    direct = [slot for slot in range(1, T) if slot == 1 or slot % 2 == 0]
    for index in range(dm.NCH):
        for slot in direct:
            weight_copy(slot, index).start()

    def relay(slot, index):
        weight_copy(slot, index).wait_recv()
        weight_copy(slot + 1, index).start()

    own_vec.wait()
    own_in.wait()
    for slot in range(1, T):
        vector_copy(slot).wait_recv()
        input_copy(slot).wait_recv()

    @pl.when(upper)
    def _():
        for index in range(dm.NCH):
            for slot in range(2, T, 2):
                relay(slot, index)
        stream_copy.wait_recv()

    @pl.when(lower)
    def _():
        load = pltpu.make_async_copy(xc, xarr, lsem.at[0])
        load.start()
        load.wait()

    def arrive(slot, index):
        if slot == 0:
            return
        if slot % 2 == 0:

            @pl.when(lower)
            def _():
                relay(slot, index)

        else:
            weight_copy(slot, index).wait_recv()

    def source_of(slot, index):
        return chunk_refs(dm, index, *(own if slot == 0 else slot_refs(slot)))

    keep_x = pltpu.make_async_copy(xarr, xkeep, lsem.at[1])
    keep_x.start()
    keep_p = pltpu.make_async_copy(spb, spkeep, lsem.at[2])
    keep_p.start()

    gain, bias = full_vector(dm, spb, LN1_GAIN), full_vector(dm, spb, LN1_BIAS)

    def first_norm(r, _):
        rows = pl.ds(pl.multiple_of(r * STEP, STEP), STEP)
        hat, _inv = norm_rows(block_rows(dm, xarr, rows).astype(F32), D)
        n1[rows, :] = (hat * gain + bias).astype(BF16)
        return 0

    lax.fori_loop(0, RP // STEP, first_norm, 0)

    for index, (slot, c) in enumerate(dm.order):
        shard = spb[partner(tensor, slot)]
        per = C // W
        first = FC1_BIAS + c * per
        b1r[index] = jnp.concatenate([shard[first + i : first + i + 1, :] for i in range(per)], axis=1)

    pad = jnp.zeros((RL - RP, W), BF16)
    for slot in range(T):
        for ref in (q, k, v):
            ref[slot, pl.ds(RP, RL - RP), :] = pad

    def load_qkv(slot, parity):
        return pltpu.make_async_copy(source_of(slot, 0), wq.at[parity], lw.at[parity])

    def fetch_qkv(which):
        for slot in range(T):

            @pl.when(which == slot)
            def _():
                arrive(slot, 0)
                load_qkv(slot, slot % 2).start()

    masks = half_masks(128)
    lane = lax.broadcasted_iota(jnp.int32, (1, RL), 1)
    key_bias = jnp.where(lane < dm.tok, 0.0, MASKED).astype(F32)

    fetch_qkv(0)

    def heads(slot, _):
        parity = lax.rem(slot, 2)
        pltpu.make_async_copy(gqkv.at[0], wq.at[parity], lw.at[parity]).wait()
        early = jnp.logical_or(upper, slot < 1)

        @pl.when(jnp.logical_and(early, slot + 1 < T))
        def _():
            fetch_qkv(slot + 1)

        shard = spb[partner_dynamic(dm, tensor, slot)]
        rows = pl.ds(0, RP)
        q[slot, rows, :] = (dot_plain(n1[...], wq[parity, 0]) + shard[Q_BIAS : Q_BIAS + 1]).astype(BF16)
        k[slot, rows, :] = dot_plain(n1[...], wq[parity, 1]).astype(BF16)
        v[slot, rows, :] = (dot_plain(n1[...], wq[parity, 2]) + shard[V_BIAS : V_BIAS + 1]).astype(BF16)

        for pair in range(W // 128):
            lanes = slice(pair * 128, pair * 128 + 128)

            def block(b, _):
                rows = pl.ds(pl.multiple_of(b * 128, 128), 128)
                query = q[slot, rows, lanes] * jnp.asarray(HEAD_DIM**-0.5, BF16)
                parts = []
                for mask in masks:
                    s = dot_last(jnp.where(mask, query, jnp.zeros_like(query)), k[slot, :, lanes]) + key_bias
                    e = jnp.exp(s - jnp.max(s, axis=1, keepdims=True))
                    p = (e * (1.0 / jnp.sum(e, axis=1, keepdims=True))).astype(BF16)
                    parts.append(dot_plain(p, v[slot, :, lanes]))
                o[slot, rows, lanes] = jnp.where(masks[0], parts[0], parts[1]).astype(BF16)
                return 0

            lax.fori_loop(0, RL // 128, block, 0, unroll=True)

        @pl.when(jnp.logical_and(jnp.logical_not(early), slot + 1 < T))
        def _():
            fetch_qkv(slot + 1)

        return 0

    lax.fori_loop(0, T, heads, 0)

    keeps = []
    for number, (source, target) in enumerate(((q, qkeep), (k, kkeep), (v, vkeep), (o, okeep))):
        keeps.append(pltpu.make_async_copy(source, target, la.at[2 + number]))
        keeps[-1].start()

    loads = []
    for slot in range(T):
        arrive(slot, 1)
        loads.append(
            pltpu.make_async_copy(source_of(slot, 1), wob.at[pl.ds(slot * W, W)], lw.at[2 + slot])
        )
        loads[-1].start()

    def arrive_ff(index):
        slot, c = dm.order[index]
        arrive(slot, 2 + 2 * c)
        arrive(slot, 3 + 2 * c)

    def load_ff(index, parity):
        slot, c = dm.order[index]
        return [
            pltpu.make_async_copy(source_of(slot, 2 + 2 * c), w1b.at[parity], lsem.at[3 + parity]),
            pltpu.make_async_copy(source_of(slot, 3 + 2 * c), w2b.at[parity], lsem.at[5 + parity]),
        ]

    def fetch_ff(which):
        for index in range(NI):

            @pl.when(which == index)
            def _():
                arrive_ff(index)
                for load in load_ff(index, index % 2):
                    load.start()

    fetch_ff(0)
    for load in loads:
        load.wait()
    attended = jnp.concatenate([o[slot, pl.ds(0, RP), :] for slot in range(T)], axis=1)
    for n in range(D // 256):
        acc[:, pl.ds(n * 256, 256)] = dot_plain(attended, wob[:, pl.ds(n * 256, 256)])

    out_bias = full_vector(dm, spb, OUT_BIAS)
    gain2, bias2 = full_vector(dm, spb, LN2_GAIN), full_vector(dm, spb, LN2_BIAS)
    down_bias = full_vector(dm, spb, FC2_BIAS)

    def second_norm(r, _):
        rows = pl.ds(pl.multiple_of(r * STEP, STEP), STEP)
        hidden = block_rows(dm, xarr, rows).astype(F32) + (acc[rows, :] + out_bias)
        hat, _inv = norm_rows(hidden, D)
        n2[rows, :] = (hat * gain2 + bias2).astype(BF16)
        acc[rows, :] = hidden
        return 0

    lax.fori_loop(0, RP // STEP, second_norm, 0)
    keep_h = pltpu.make_async_copy(acc, hkeep, lsem.at[0])
    keep_h.start()
    keep_h.wait()

    def keep_a(index, parity):
        return pltpu.make_async_copy(ab.at[parity], akeep.at[index], la.at[parity])

    def feed(index, _):
        parity = lax.rem(index, 2)
        for load in load_ff(0, parity):
            load.wait()
        early = jnp.logical_or(upper, index + 1 < 2 * dm.NC)

        @pl.when(jnp.logical_and(early, index + 1 < NI))
        def _():
            fetch_ff(index + 1)

        @pl.when(index >= 2)
        def _():
            keep_a(index - 2, parity).wait()

        ab[parity] = dot_plain(n2[...], w1b[parity])
        shift = b1r[index]

        def bend(r, _):
            rows = pl.ds(pl.multiple_of(r * STEP, STEP), STEP)
            a = ab[parity, rows, :] + shift
            ab[parity, rows, :] = a
            gb[rows, :] = (0.5 * a * (1.0 + lax.erf(a * ROOT_HALF))).astype(BF16)
            return 0

        lax.fori_loop(0, RP // STEP, bend, 0)
        keep_a(index, parity).start()
        for n in range(D // 256):
            cols = pl.ds(n * 256, 256)
            acc[:, cols] += dot_plain(gb[...], w2b[parity, :, cols])

        @pl.when(jnp.logical_and(jnp.logical_not(early), index + 1 < NI))
        def _():
            fetch_ff(index + 1)

        return 0

    lax.fori_loop(0, NI, feed, 0)

    def close(r, _):
        rows = pl.ds(pl.multiple_of(r * STEP, STEP), STEP)
        y = (acc[rows, :] + down_bias).astype(BF16)
        for j in range(T):
            yb[j, rows, :] = y[:, j * W : (j + 1) * W]
        return 0

    lax.fori_loop(0, RP // STEP, close, 0)

    @pl.when(lower)
    def _():
        stream_copy.start()

    for slot in range(1, T):
        output_copy(slot).start()
    own_out = pltpu.make_async_copy(yb.at[tensor], result.at[tensor], lsem.at[0])
    own_out.start()
    own_out.wait()
    keep_x.wait()
    keep_p.wait()
    for keep in keeps:
        keep.wait()
    for index in (NI - 2, NI - 1):
        keep_a(index, index % 2).wait()
    for slot in range(1, T):
        output_copy(slot).wait()
        vector_copy(slot).wait_send()
        input_copy(slot).wait_send()
        for index in range(dm.NCH):
            weight_copy(slot, index).wait_send()

    @pl.when(lower)
    def _():
        stream_copy.wait_send()


def partner_dynamic(dm, place, slot):
    bit = 1
    while bit < dm.T:
        take = lax.rem(lax.div(slot, bit), 2)
        place = place + take * (bit - 2 * bit * lax.rem(lax.div(place, bit), 2))
        bit *= 2
    return place


def forward_call(dm, xin, vectors, wqkv, wout, wup, wdown):
    T, W, D, RP, RL, C, NI, FL = dm.T, dm.W, dm.D, dm.RP, dm.RL, dm.C, dm.NI, dm.FL
    sds = jax.ShapeDtypeStruct
    outs = (
        sds((T, 3, D, W), BF16), sds((T, W, D), BF16), sds((T, D, FL), BF16), sds((T, FL, D), BF16),
        sds((T, RP, W), BF16), sds((T, RP, W), BF16),
        sds((T, RL, W), BF16), sds((T, RL, W), BF16), sds((T, RL, W), BF16), sds((T, RL, W), BF16),
        sds((RP, D), F32), sds((NI, RP, C), F32), sds((T, VECTOR_ROWS, W), F32), sds((T, RP, W), BF16),
    )
    dma = pltpu.SemaphoreType.DMA
    scratch = [
        pltpu.VMEM((T, RP, W), BF16), pltpu.VMEM((RP, D), BF16), pltpu.VMEM((2, 3, D, W), BF16),
        pltpu.VMEM((D, D), BF16), pltpu.VMEM((2, D, C), BF16), pltpu.VMEM((2, C, D), BF16),
        pltpu.VMEM((2, RP, C), F32), pltpu.VMEM((RP, C), BF16), pltpu.VMEM((RP, D), F32),
        pltpu.VMEM((RP, D), BF16), pltpu.VMEM((T, RP, W), BF16), pltpu.VMEM((NI, 1, C), F32),
        pltpu.VMEM((T, VECTOR_ROWS, W), F32),
        pltpu.VMEM((T, RL, W), BF16), pltpu.VMEM((T, RL, W), BF16), pltpu.VMEM((T, RL, W), BF16), pltpu.VMEM((T, RL, W), BF16),
        dma((T, dm.NCH)), dma((T, dm.NCH)), dma((T,)), dma((T,)), dma((T,)), dma((T,)), dma((T,)), dma((T,)),
        dma((2,)), dma((8,)), dma((2 + T,)), dma((6,)),
    ]
    return pl.pallas_call(
        functools.partial(forward_kernel, dm),
        out_shape=outs,
        in_specs=[ANY] * 6,
        out_specs=[ANY] * len(outs),
        scratch_shapes=scratch,
        name="layer_forward",
        compiler_params=pltpu.CompilerParams(
            collective_id=0, has_side_effects=True, vmem_limit_bytes=VMEM_BYTES
        ),
    )(xin, vectors, wqkv, wout, wup, wdown)


def packed_vectors(dm, ln1_gain, ln1_bias, qv_bias, out_bias, ln2_gain, ln2_bias, fc1_bias, fc2_bias):
    rows = [ln1_gain, ln1_bias, qv_bias[0], out_bias, ln2_gain, ln2_bias, fc2_bias, fc1_bias]
    flat = jnp.concatenate([row.reshape(-1, dm.W) for row in rows], axis=0)
    return jnp.pad(flat, ((0, VECTOR_ROWS - flat.shape[0]), (0, 0)))


def padded_rows(dm, array):
    return jnp.pad(array, ((0, 0), (0, dm.RP - dm.tok), (0, 0)))


def dot_rows(left, right):
    return lax.dot_general(left, right, (((0,), (0,)), ((), ())), preferred_element_type=F32)


def fold(rows):
    total = rows[0:8, :]
    for first in range(8, rows.shape[0], 8):
        total = total + rows[first : first + 8, :]
    return total


def norm_rows_back(grad, hat, inv, gain, width):
    scaled = grad * gain
    mean = jnp.sum(scaled, axis=1, keepdims=True) * (1.0 / width)
    along = jnp.sum(scaled * hat, axis=1, keepdims=True) * (1.0 / width)
    return inv * (scaled - mean - hat * along)


def backward_kernel(
    dm,
    xc, xkeep, qkeep, kkeep, vkeep, okeep, hkeep, akeep, spkeep,
    wqkv, wout, wup, wdown, gqkv, gout, gup, gdown,
    dqkv, dout, dup, ddown, result, flat_sums, head_sums, up_sums,
    arr, dyb, acc, dh, hh, dhb, gs, das, n1t, n2t, nb, q, k, v, o, do, dq, dk, dv, xx,
    w1b, w2b, ab, dgb, wob, wq, s1, s2, yb, spb, fs, hs, us, dva, dka,
    ssem, osend, orecv, lsem, lw, lq, lg,
):
    section, tensor = lax.axis_index("section"), lax.axis_index("tensor")
    T, W, D, RP, RL, C, NI = dm.T, dm.W, dm.D, dm.RP, dm.RL, dm.C, dm.NI
    lower, upper = section == 0, section == 1
    own = (wqkv, wout, wup, wdown)
    real = pl.ds(0, RP)

    def source_of(slot, index):
        if slot == 0:
            return chunk_refs(dm, index, *own)
        return chunk_refs(dm, index, gqkv.at[slot], gout.at[slot], gup.at[slot], gdown.at[slot])

    stream_copy = pltpu.make_async_remote_copy(
        src_ref=arr,
        dst_ref=arr,
        send_sem=ssem.at[0],
        recv_sem=ssem.at[1],
        device_id={"section": 1 - section},
    )

    def output_copy(slot):
        return pltpu.make_async_remote_copy(
            src_ref=yb.at[partner(tensor, slot)],
            dst_ref=result.at[tensor],
            send_sem=osend.at[slot],
            recv_sem=orecv.at[slot],
            device_id={"tensor": partner(tensor, slot)},
        )

    def load_ff(index, parity):
        slot, c = dm.order[index]
        return [
            pltpu.make_async_copy(source_of(slot, 2 + 2 * c), w1b.at[parity], lw.at[parity]),
            pltpu.make_async_copy(source_of(slot, 3 + 2 * c), w2b.at[parity], lw.at[2 + parity]),
            pltpu.make_async_copy(akeep.at[index], ab.at[parity], lw.at[4 + parity]),
        ]

    def fetch_ff(which):
        for index in range(NI):

            @pl.when(which == index)
            def _():
                for load in load_ff(index, index % 2):
                    load.start()

    fetch_ff(0)
    loads = [
        pltpu.make_async_copy(source, target, lsem.at[number])
        for number, (source, target) in enumerate(
            ((spkeep, spb), (hkeep, hh), (qkeep, q), (kkeep, k), (vkeep, v), (okeep, o), (xkeep, xx))
        )
    ]
    for load in loads:
        load.start()
    out_loads = [
        pltpu.make_async_copy(source_of(slot, 1), wob.at[pl.ds(slot * W, W)], lq.at[2 + slot])
        for slot in range(T)
    ]
    for load in out_loads:
        load.start()

    meet(dm, section, tensor)

    @pl.when(upper)
    def _():
        load = pltpu.make_async_copy(xc, arr, lsem.at[7])
        load.start()
        load.wait()

    tail_rows = pl.ds(RP, RL - RP)
    blank = jnp.zeros((RL - RP, D), BF16)
    dyb[tail_rows, :] = blank
    dhb[tail_rows, :] = blank
    nb[tail_rows, :] = blank
    for index in range(NI):
        gs[index, tail_rows, :] = blank[:, :C]
        das[index, tail_rows, :] = blank[:, :C]
    for slot in range(T):
        do[slot, tail_rows, :] = blank[:, :W]
    acc[...] = jnp.zeros_like(acc)
    fs[...] = jnp.zeros_like(fs)
    hs[...] = jnp.zeros_like(hs)

    @pl.when(lower)
    def _():
        stream_copy.wait_recv()

    def spread(r, _):
        rows = pl.ds(pl.multiple_of(r * STEP, STEP), STEP)
        dyb[rows, :] = block_rows(dm, arr, rows)
        return 0

    lax.fori_loop(0, RP // STEP, spread, 0)

    def feed_back(index, _):
        parity = lax.rem(index, 2)
        for load in load_ff(0, parity):
            load.wait()

        @pl.when(index + 1 < NI)
        def _():
            fetch_ff(index + 1)

        dgb[...] = dot_last(dyb[real, :], w2b[parity])

        def bend(r, total):
            rows = pl.ds(pl.multiple_of(r * STEP, STEP), STEP)
            a = ab[parity, rows, :]
            cdf = 0.5 * (1.0 + lax.erf(a * ROOT_HALF))
            gs[index, rows, :] = (a * cdf).astype(BF16)
            da = dgb[rows, :] * (cdf + a * jnp.exp(-0.5 * a * a) * GAUSS_FACTOR)
            das[index, rows, :] = da.astype(BF16)
            return total + fold(da)

        total = lax.fori_loop(0, RP // STEP, bend, jnp.zeros((8, C), F32))
        us[index] = jnp.sum(total, axis=0, keepdims=True)
        for n in range(D // 256):
            cols = pl.ds(n * 256, 256)
            acc[:, cols] += dot_last(das[index, real, :], w1b[parity, cols, :])
        return 0

    lax.fori_loop(0, NI, feed_back, 0)

    for load in loads:
        load.wait()
    for load in out_loads:
        load.wait()
    gain2, bias2 = full_vector(dm, spb, LN2_GAIN), full_vector(dm, spb, LN2_BIAS)

    def second_norm(r, _):
        rows = pl.ds(pl.multiple_of(r * STEP, STEP), STEP)
        hat, inv = norm_rows(hh[rows, :], D)
        grad = acc[rows, :]
        dy = dyb[rows, :].astype(F32)
        fs[0] += fold(grad * hat)
        fs[1] += fold(grad)
        whole = dy + norm_rows_back(grad, hat, inv, gain2, D)
        dh[rows, :] = whole
        dhb[rows, :] = whole.astype(BF16)
        fs[2] += fold(whole)
        fs[3] += fold(dy)
        nb[rows, :] = (hat * gain2 + bias2).astype(BF16)
        return 0

    lax.fori_loop(0, RP // STEP, second_norm, 0)

    def turn(target):
        for n in range(D // 256):
            cols = pl.ds(n * 256, 256)
            target[cols, :] = nb[:, cols].T

    turn(n2t)

    def put_ff(index, parity):
        slot, c = dm.order[index]
        return [
            pltpu.make_async_copy(s1.at[parity], dup.at[slot, :, pl.ds(c * C, C)], lg.at[parity]),
            pltpu.make_async_copy(s2.at[parity], ddown.at[slot, pl.ds(c * C, C), :], lg.at[2 + parity]),
        ]

    def feed_weights():
        def one(index, _):
            parity = lax.rem(index, 2)

            @pl.when(index >= 2)
            def _():
                for put in put_ff(0, parity):
                    put.wait()

            for n in range(D // 256):
                cols = pl.ds(n * 256, 256)
                s1[parity, cols, :] = dot_plain(n2t[cols, :], das[index]).astype(BF16)
            for n in range(C // 256):
                cols = pl.ds(n * 256, 256)
                s2[parity, cols, :] = dot_rows(gs[index, :, cols], dyb[...]).astype(BF16)
            for j in range(NI):

                @pl.when(index == j)
                def _():
                    for put in put_ff(j, j % 2):
                        put.start()

            return 0

        lax.fori_loop(0, NI, one, 0)
        for parity in range(2):
            for put in put_ff(0, parity):
                put.wait()

    @pl.when(lower)
    def _():
        feed_weights()

    for slot in range(T):
        do[slot, real, :] = dot_last(dhb[real, :], wob[pl.ds(slot * W, W), :]).astype(BF16)

    mask_full = half_masks(RL)
    row = lax.broadcasted_iota(jnp.int32, (RL, 1), 0)
    key_bias = jnp.where(row < dm.tok, 0.0, MASKED).astype(F32)
    scale = HEAD_DIM**-0.5
    blocks = [(first, min(256, RL - first)) for first in range(0, RL, 256)]

    def heads(slot, _):
        for pair in range(W // 128):
            lanes = slice(pair * 128, pair * 128 + 128)
            keys, values = k[slot, :, lanes], v[slot, :, lanes]
            for number, (first, size) in enumerate(blocks):
                rows = slice(first, first + size)
                query, grad = q[slot, rows, lanes], do[slot, rows, lanes]
                dq_block = jnp.zeros((size, 128), F32)
                dk_block, dv_block = jnp.zeros((RL, 128), F32), jnp.zeros((RL, 128), F32)
                for half in range(2):
                    mask = mask_full[half][:size]
                    query_h = jnp.where(mask, query, jnp.zeros_like(query))
                    grad_h = jnp.where(mask, grad, jnp.zeros_like(grad))
                    keys_h = jnp.where(mask_full[half], keys, jnp.zeros_like(keys))
                    s = dot_last(keys, query_h * jnp.asarray(scale, BF16)) + key_bias
                    e = jnp.exp(s - jnp.max(s, axis=0, keepdims=True))
                    p = e * (1.0 / jnp.sum(e, axis=0, keepdims=True))
                    dp = dot_last(values, grad_h)
                    delta = jnp.sum(p * dp, axis=0, keepdims=True)
                    ds = (p * (dp - delta) * scale).astype(BF16)
                    dv_block = dv_block + dot_plain(p.astype(BF16), grad_h)
                    dk_block = dk_block + dot_plain(ds, query_h)
                    dq_block = dq_block + dot_rows(ds, keys_h)
                dq[slot, rows, lanes] = dq_block.astype(BF16)
                hs[slot, 0, :, lanes] += fold(dq_block)
                if number == 0:
                    dka[...] = dk_block
                    dva[...] = dv_block
                else:
                    dka[...] += dk_block
                    dva[...] += dv_block
            dk[slot, :, lanes] = dka[...].astype(BF16)
            total = dva[...]
            dv[slot, :, lanes] = total.astype(BF16)
            hs[slot, 1, :, lanes] += fold(total)
        return 0

    lax.fori_loop(0, T, heads, 0)

    def load_qkv(slot, parity):
        return pltpu.make_async_copy(source_of(slot, 0), wq.at[parity], lq.at[parity])

    load_qkv(0, 0).start()
    for slot in range(T):
        load_qkv(slot, slot % 2).wait()
        if slot + 1 < T:
            load_qkv(slot + 1, (slot + 1) % 2).start()
        for n in range(D // 256):
            cols = pl.ds(n * 256, 256)
            part = dot_last(dq[slot, real, :], wq[slot % 2, 0, cols, :])
            part = part + dot_last(dk[slot, real, :], wq[slot % 2, 1, cols, :])
            part = part + dot_last(dv[slot, real, :], wq[slot % 2, 2, cols, :])
            if slot == 0:
                acc[:, cols] = part
            else:
                acc[:, cols] += part

    gain1, bias1 = full_vector(dm, spb, LN1_GAIN), full_vector(dm, spb, LN1_BIAS)

    def first_norm(r, _):
        rows = pl.ds(pl.multiple_of(r * STEP, STEP), STEP)
        hat, inv = norm_rows(block_rows(dm, xx, rows).astype(F32), D)
        grad = acc[rows, :]
        fs[4] += fold(grad * hat)
        fs[5] += fold(grad)
        whole = dh[rows, :] + norm_rows_back(grad, hat, inv, gain1, D)
        nb[rows, :] = (hat * gain1 + bias1).astype(BF16)
        low = whole.astype(BF16)
        for j in range(T):
            yb[j, rows, :] = whole[:, j * W : (j + 1) * W]
            xx[j, rows, :] = low[:, j * W : (j + 1) * W]
        return 0

    lax.fori_loop(0, RP // STEP, first_norm, 0)

    down_copy = pltpu.make_async_remote_copy(
        src_ref=xx,
        dst_ref=arr,
        send_sem=ssem.at[0],
        recv_sem=ssem.at[1],
        device_id={"section": 1 - section},
    )

    @pl.when(upper)
    def _():
        down_copy.start()

    for slot in range(1, T):
        output_copy(slot).start()
    own_out = pltpu.make_async_copy(yb.at[tensor], result.at[tensor], lsem.at[0])
    own_out.start()
    turn(n1t)

    def put_qkv(slot, parity):
        return [
            pltpu.make_async_copy(s1.at[parity, :, pl.ds(0, W)], dqkv.at[slot, 0], lg.at[4 + parity]),
            pltpu.make_async_copy(s1.at[parity, :, pl.ds(C // 2, W)], dqkv.at[slot, 1], lg.at[6 + parity]),
        ]

    for slot in range(T):
        number = 0
        s2[slot % 2, pl.ds(0, W), :] = dot_rows(o[slot], dhb[...]).astype(BF16)
        put_out = pltpu.make_async_copy(s2.at[slot % 2, pl.ds(0, W), :], dout.at[slot], lg.at[4])
        put_out.start()
        for source in (dq, dk, dv):
            for n in range(D // 256):
                cols = pl.ds(n * 256, 256)
                s1[number % 2, cols, pl.ds(0, W)] = dot_plain(n1t[cols, :], source[slot]).astype(BF16)
            put = pltpu.make_async_copy(s1.at[number % 2, :, pl.ds(0, W)], dqkv.at[slot, number], lg.at[number % 2])
            put.start()
            put.wait()
            number += 1
        put_out.wait()

    @pl.when(upper)
    def _():
        feed_weights()

    keeps = []
    for number, (source, target) in enumerate(((fs, flat_sums), (hs, head_sums), (us, up_sums))):
        keeps.append(pltpu.make_async_copy(source, target, lsem.at[1 + number]))
        keeps[-1].start()
    for keep in keeps:
        keep.wait()
    own_out.wait()
    for slot in range(1, T):
        output_copy(slot).wait()

    @pl.when(upper)
    def _():
        down_copy.wait_send()


def backward_call(dm, kept, own):
    T, W, D, RP, RL, C, NI, FL = dm.T, dm.W, dm.D, dm.RP, dm.RL, dm.C, dm.NI, dm.FL
    sds = jax.ShapeDtypeStruct
    gathered, rest = kept[:4], kept[4:13]
    outs = (
        sds((T, 3, D, W), BF16), sds((T, W, D), BF16), sds((T, D, FL), BF16), sds((T, FL, D), BF16),
        sds((T, RP, W), F32), sds((6, 8, D), F32), sds((T, 2, 8, W), F32), sds((NI, 1, C), F32),
    )
    dma = pltpu.SemaphoreType.DMA
    heads = pltpu.VMEM((T, RL, W), BF16)
    scratch = [
        pltpu.VMEM((T, RP, W), BF16), pltpu.VMEM((RL, D), BF16), pltpu.VMEM((RP, D), F32), pltpu.VMEM((RP, D), F32),
        pltpu.VMEM((RP, D), F32), pltpu.VMEM((RL, D), BF16), pltpu.VMEM((NI, RL, C), BF16), pltpu.VMEM((NI, RL, C), BF16),
        pltpu.VMEM((D, RL), BF16), pltpu.VMEM((D, RL), BF16), pltpu.VMEM((RL, D), BF16),
        heads, heads, heads, heads, heads, heads, heads, heads, pltpu.VMEM((T, RP, W), BF16),
        pltpu.VMEM((2, D, C), BF16), pltpu.VMEM((2, C, D), BF16), pltpu.VMEM((2, RP, C), F32), pltpu.VMEM((RP, C), F32),
        pltpu.VMEM((D, D), BF16), pltpu.VMEM((2, 3, D, W), BF16), pltpu.VMEM((2, D, C), BF16), pltpu.VMEM((2, C, D), BF16),
        pltpu.VMEM((T, RP, W), F32), pltpu.VMEM((T, VECTOR_ROWS, W), F32),
        pltpu.VMEM((6, 8, D), F32), pltpu.VMEM((T, 2, 8, W), F32), pltpu.VMEM((NI, 1, C), F32),
        pltpu.VMEM((RL, 128), F32), pltpu.VMEM((RL, 128), F32),
        dma((2,)), dma((T,)), dma((T,)), dma((8,)), dma((6,)), dma((2 + T,)), dma((8,)),
    ]
    return pl.pallas_call(
        functools.partial(backward_kernel, dm),
        out_shape=outs,
        in_specs=[ANY] * 17,
        out_specs=[ANY] * len(outs),
        scratch_shapes=scratch,
        name="layer_backward",
        compiler_params=pltpu.CompilerParams(
            collective_id=1, has_side_effects=True, vmem_limit_bytes=VMEM_BYTES
        ),
    )(*rest, *own, *gathered)


def shards(
    images, cotangent, ln1_gain, ln1_bias, qkv_weight, qv_bias, out_weight, out_bias,
    ln2_gain, ln2_bias, fc1_weight, fc1_bias, fc2_weight, fc2_bias,
):
    dm = sizes_of(images, fc1_weight, lax.axis_size("tensor"))
    T, W, D = dm.T, dm.W, dm.D
    section, tensor = lax.axis_index("section"), lax.axis_index("tensor")
    xin = padded_rows(dm, jnp.where(section == 0, images[:, 0], cotangent[:, 0]))
    vectors = packed_vectors(
        dm, ln1_gain[0], ln1_bias[0], qv_bias, out_bias[0], ln2_gain[0], ln2_bias[0], fc1_bias[0], fc2_bias[0]
    )
    own = (qkv_weight[0], out_weight[0], fc1_weight[0], fc2_weight[0])
    kept = forward_call(dm, xin, vectors, *own)
    section_out = kept[13][: dm.micro, : dm.tok][None, :, None]
    dqkv, dout, dup, ddown, result, flat_sums, head_sums, up_sums = backward_call(dm, kept, own)
    input_grads = result[: dm.micro, : dm.tok][None, :, None]

    def reduced(parts):
        if T > dm.micro:
            parts = jnp.where(tensor < dm.micro, parts, jnp.zeros_like(parts))
        bit = 1
        while bit < T:
            keep = [slot for slot in range(parts.shape[0]) if slot % 2 == 0]
            give = [slot for slot in range(parts.shape[0]) if slot % 2 == 1]
            pairs = [(source, source ^ bit) for source in range(T)]
            sent = lax.ppermute(parts[jnp.array(give)], "tensor", pairs)
            parts = parts[jnp.array(keep)].astype(F32) + sent.astype(F32)
            if parts.shape[0] > 1 or True:
                parts = parts.astype(BF16)
            bit *= 2
        return lax.psum(parts[0], "dp").astype(F32)

    absolute = jnp.sum(flat_sums, axis=1).reshape(6, T, W)
    by_slot = jnp.sum(head_sums, axis=2)
    up_rows = [None] * T
    for index, (slot, c) in enumerate(dm.order):
        up_rows[slot] = (up_rows[slot] or []) + [up_sums[index].reshape(-1, W)]
    by_slot = jnp.concatenate([by_slot, jnp.stack([jnp.concatenate(rows, axis=0) for rows in up_rows])], axis=1)
    places = jnp.stack([partner(tensor, slot) for slot in range(T)])
    relative = jnp.zeros_like(by_slot).at[places].set(by_slot)
    small = jnp.concatenate([absolute.transpose(1, 0, 2), relative], axis=1)
    if T > dm.micro:
        small = jnp.where(tensor < dm.micro, small, jnp.zeros_like(small))
    small = lax.psum(small, ("tensor", "dp"))
    small = lax.dynamic_index_in_dim(small, tensor, 0, keepdims=False)
    g2, b2, ob, db, g1, b1 = (small[i][None] for i in range(6))
    qv = small[6:8][None]
    ub = small[8:].reshape(1, -1)
    return (
        section_out, input_grads, g1, b1, reduced(dqkv)[None], qv, reduced(dout)[None], ob, g2, b2,
        reduced(dup)[None], ub, reduced(ddown)[None], db,
    )


def solution(mesh):
    vector = P("section", "tensor")
    rows = P(None, "dp", None, "tensor")
    placed_rows = P("section", None, "dp", None, "tensor")
    qkv, qv = P("section", None, None, "tensor"), P("section", None, "tensor")
    by_row, by_column = P("section", "tensor", None), P("section", None, "tensor")
    return jax.shard_map(
        shards,
        mesh=mesh,
        in_specs=(rows, rows, vector, vector, qkv, qv, by_row, vector, vector, vector, by_column, vector, by_row, vector),
        out_specs=(
            placed_rows, placed_rows, vector, vector, qkv, qv, by_row, vector, vector, vector,
            by_column, vector, by_row, vector,
        ),
        check_vma=False,
    )
```

profile of v0, /device:TPU:0, one launch (start us, length us, event | category | flops | bytes accessed | tf_op | source)
XLA Modules:
  0.0 951.6 jit_solution(10900841285135619397)
XLA Ops:
  14.2 188.8 %layer_forward.1 = (bf16[4,3,1024,256]{3,2,1,0:T(8,128)(2,1)}, bf16[4,256,1024]{2,1,0:T(8,128)(2,1)}, bf16[4,1024,1024]{2,1,0:T(8,128)(2,1)}, bf16[4,1024,1024]{...) custom-call(bf16[4,608,256]{2,1,0:T(8,128)(2,1)} %pad.8.xin, ...), custom_call_target="tpu_custom_call" | custom-call | tf_op jit(solution)/shard_map/layer_forward/pallas_call | solution.py:462
  203.0 291.5 %layer_backward.1 = (bf16[4,3,1024,256]{3,2,1,0:T(8,128)(2,1)}, bf16[4,256,1024]{2,1,0:T(8,128)(2,1)}, bf16[4,1024,1024]{2,1,0:T(8,128)(2,1)}, bf16[4,1024,1024]...) custom-call(bf16[4,608,256]{2,1,0:T(8,128)(2,1)} %get-tuple-element., ...), custom_call_target="tpu_custom_call" | custom-call | tf_op jit(solution)/shard_map/layer_backward/pallas_call | solution.py:868
  494.6 12.6 %fusion.8 = (bf16[4,512,1024]{2,1,0:T(8,128)(2,1)}, bf16[4,512,1024]{2,1,0:T(8,128)(2,1)}, bf16[4,512,1024]{2,1,0:T(8,128)(2,1)}, bf16[4,512,1024]{2,1,0:T(8,128)(2,1)}) fusion(bf16[4,1024,1024]{2,1,0:T(8,128)(2,1)} %get-tuple-element.57, bf16[4,1024,1024]{2,1,0:T(8,128)(2,1)} %get-tuple-element.56), kind=kLoop, calls=%fused_computation.60 | loop fusion | bytes 33554432 | tf_op jit(solution)/shard_map/gather | solution.py:907
  507.1 2.9 gather_fusion.7
  510.0 4.2 gather_fusion.6
  514.2 4.0 pad_maximum_fusion
  518.6 2.9 gather_fusion.11
  521.4 4.2 gather_fusion.10
  525.6 4.0 pad_maximum_fusion.1
  529.7 5.3 gather_fusion.1
  537.2 3.5 gather_fusion
  540.7 4.2 gather_fusion.5
  544.9 4.2 gather_fusion.4
  549.1 4.2 gather_fusion.9
  553.3 4.2 gather_fusion.8
  563.5 3.6 add_convert_fusion.1
  571.6 3.9 add_convert_fusion
  584.2 115.3 %collective-permute-done.3 = bf16[1,256,1024]{2,1,0:T(8,128)(2,1)S(1)} collective-permute-done((bf16[1,256,1024]{2,1,0:T(8,128)(2,1)S(1)}, bf16[1,256,1024]{2,1,0:T(8,128)(2,1)S(1)}, u32[]{:S(2)}, u32[]{:S(2)}) %collective-permute-start.3) | collective-permute-done | bytes 524320 | tf_op jit(solution)/shard_map/ppermute | solution.py:906
  700.6 3.2 add_convert_fusion.5
  706.6 3.9 add_convert_fusion.3
  713.7 3.8 copy.51
  718.6 72.8 %psum.35 = f32[4,12,256]{2,1,0:T(8,128)S(1)} all-reduce(f32[4,12,256]{2,1,0:T(8,128)S(1)} %pad_maximum_fusion.2), channel_id=1, replica_groups=mesh['section'=2,'dp'=4,'tensor'=4] {'tensor','dp'}, use_global_device_ids=true, to_apply=%region_3.4 | all-reduce | flops 12288 | bytes 98304 | tf_op jit(solution)/shard_map/psum | solution.py:924
  793.2 141.8 %all-reduce.5.cloned.1.call-done = (bf16[1,3,1024,256]{3,2,1,0:T(8,128)(2,1)}, bf16[1,256,1024]{2,1,0:T(8,128)(2,1)}, bf16[1,1024,1024]{2,1,0:T(8,128)(2,1)}, bf16[1,1024,1024]{2,1,0:T(8,128)(2,1)}) async-done(((bf16[1,3,1024,256]{3,2,1,0:T(8,128)(2,1)}, bf16[1,256,1024]{2,1,0:T(8,128)(2,1)}, bf16[1,1024,1024]{2,1,0:T(8,128)(2,1)}, bf16[1,1024,1024]{2,1,0:T(8,128)(2,1)}), ...) | async-done | bytes 6291472 | tf_op jit(solution)/shard_map/psum | solution.py:911
  935.0 3.5 broadcast_in_dim.91
  (117 shorter events, 44.5 us)
Async XLA Ops:
  7.2 927.8 %all-reduce.5.cloned.1.call-start = ((), (), s32[]{:S(2)}) async-start(), calls=%async_computation | async-start | bytes 12582912 | tf_op jit(solution)/shard_map/psum | solution.py:911
  10.4 3.2 copy-start.22
  10.4 3.2 copy-start.23
  494.6 12.6 %copy-start.18 = (s32[1024]{0:T(1024)S(1)}, s32[1024]{0:T(1024)}, u32[]{:S(2)}) copy-start(s32[1024]{0:T(1024)} %pad_clamp_fusion) | copy-start | bytes 12292
  518.2 44.7 %collective-permute-start.4 = (bf16[2,1024,1024]{2,1,0:T(8,128)(2,1)}, bf16[2,1024,1024]{2,1,0:T(8,128)(2,1)}, u32[]{:S(2)}, u32[]{:S(2)}) collective-permute-start(bf16[2,1024,1024]{2,1,0:T(8,128)(2,1)} %pad_maximum_fusion), channel_id=1, source_target_pairs={{0,1},{1,0},{2,3},{3,2},{4,5},{5,4},{6,7},{7,6},{8,9},{9,8},{10,11... | collective-permute-start | bytes 12582920 | tf_op jit(solution)/shard_map/ppermute | solution.py:906
  529.6 40.3 %collective-permute-start.6 = (bf16[2,1024,1024]{2,1,0:T(8,128)(2,1)}, bf16[2,1024,1024]{2,1,0:T(8,128)(2,1)}, u32[]{:S(2)}, u32[]{:S(2)}) collective-permute-start(bf16[2,1024,1024]{2,1,0:T(8,128)(2,1)} %pad_maximum_fusion.1), channel_id=1, source_target_pairs={{0,1},{1,0},{2,3},{3,2},{4,5},{5,4},{6,7},{7,6},{8,9},{9,8},{10,11... | collective-permute-start | bytes 12582920 | tf_op jit(solution)/shard_map/ppermute | solution.py:906
  529.7 5.7 copy-start.13
  535.1 22.4 %collective-permute-start = (bf16[2,3,1024,256]{3,2,1,0:T(8,128)(2,1)}, bf16[2,3,1024,256]{3,2,1,0:T(8,128)(2,1)}, u32[]{:S(2)}, u32[]{:S(2)}) collective-permute-start(bf16[2,3,1024,256]{3,2,1,0:T(8,128)(2,1)} %gather_fusion.1), channel_id=1, source_target_pairs={{0,1},{1,0},{2,3},{3,2},{4,5},{5,4},{6,7},{7,6},{8,9},{9,8},{10,11... | collective-permute-start | bytes 9437192 | tf_op jit(solution)/shard_map/ppermute | solution.py:906
  537.1 44.5 %collective-permute-start.2 = (bf16[2,256,1024]{2,1,0:T(8,128)(2,1)}, bf16[2,256,1024]{2,1,0:T(8,128)(2,1)}, u32[]{:S(2)}, u32[]{:S(2)}) collective-permute-start(bf16[2,256,1024]{2,1,0:T(8,128)(2,1)} %gather_fusion.3), channel_id=1, source_target_pairs={{0,1},{1,0},{2,3},{3,2},{4,5},{5,4},{6,7},{7,6},{8,9},{9,8},{10,11... | collective-permute-start | bytes 3145736 | tf_op jit(solution)/shard_map/ppermute | solution.py:906
  557.5 5.3 copy-start.9
  560.3 6.8 copy-start.4
  561.6 139.0 %collective-permute-start.1 = (bf16[1,3,1024,256]{3,2,1,0:T(8,128)(2,1)}, bf16[1,3,1024,256]{3,2,1,0:T(8,128)(2,1)}, u32[]{:S(2)}, u32[]{:S(2)}) collective-permute-start(bf16[1,3,1024,256]{3,2,1,0:T(8,128)(2,1)} %slice.207), channel_id=1, source_target_pairs={{0,2},{1,3},{2,0},{3,1},{4,6},{5,7},{6,4},{7,5},{8,10},{9,11},{10,... | collective-permute-start | bytes 4718600 | tf_op jit(solution)/shard_map/ppermute | solution.py:906
  567.1 8.3 copy-start
  567.2 4.4 copy-start.7
  568.7 135.1 %collective-permute-start.5 = (bf16[1,1024,1024]{2,1,0:T(8,128)(2,1)}, bf16[1,1024,1024]{2,1,0:T(8,128)(2,1)S(1)}, u32[]{:S(2)}, u32[]{:S(2)}) collective-permute-start(bf16[1,1024,1024]{2,1,0:T(8,128)(2,1)} %slice.211), channel_id=1, source_target_pairs={{0,2},{1,3},{2,0},{3,1},{4,6},{5,7},{6,4},{7,5},{8,10},{9,11},{10,... | collective-permute-start | bytes 6291464 | tf_op jit(solution)/shard_map/ppermute | solution.py:906
  578.1 128.0 %collective-permute-start.7 = (bf16[1,1024,1024]{2,1,0:T(8,128)(2,1)}, bf16[1,1024,1024]{2,1,0:T(8,128)(2,1)}, u32[]{:S(2)}, u32[]{:S(2)}) collective-permute-start(bf16[1,1024,1024]{2,1,0:T(8,128)(2,1)} %slice.213), channel_id=1, source_target_pairs={{0,2},{1,3},{2,0},{3,1},{4,6},{5,7},{6,4},{7,5},{8,10},{9,11},{10,... | collective-permute-start | bytes 6291464 | tf_op jit(solution)/shard_map/ppermute | solution.py:906
  581.6 119.0 %copy-start.5 = (bf16[2,3,1024,256]{3,2,1,0:T(8,128)(2,1)S(1)}, bf16[2,3,1024,256]{3,2,1,0:T(8,128)(2,1)}, u32[]{:S(2)}) copy-start(bf16[2,3,1024,256]{3,2,1,0:T(8,128)(2,1)} %copy-done.4) | copy-start | bytes 9437188
  583.4 116.2 %collective-permute-start.3 = (bf16[1,256,1024]{2,1,0:T(8,128)(2,1)S(1)}, bf16[1,256,1024]{2,1,0:T(8,128)(2,1)S(1)}, u32[]{:S(2)}, u32[]{:S(2)}) collective-permute-start(bf16[1,256,1024]{2,1,0:T(8,128)(2,1)S(1)} %slice.209), channel_id=1, source_target_pairs={{0,2},{1,3},{2,0},{3,1},{4,6},{5,7},{6,4},{7,5},{8,10},{9,11},{10,... | collective-permute-start | bytes 1572872 | tf_op jit(solution)/shard_map/ppermute | solution.py:906
  700.6 3.2 copy-start.1
  713.7 3.9 copy-start.17
  713.7 4.0 copy-start.16
  713.7 4.1 copy-start.15
  935.0 3.5 copy-start.14
  935.0 4.6 copy-start.12
  (11 other events, 33.1 us)
Sparse Core Ops, SparseCore 0:
  710.6 224.3 all-reduce.4
where the time goes:
time: 961 us; the launch traced here: 952 us
  Pallas kernels  480 us (50%)
  waiting for transfers between devices  257 us (27%)
  local copies, waits for them, and re-layouts  76.3 us (8%)
  blocking collectives  72.8 us (8%)
  other arithmetic  44.7 us (5%)
  between operations  14.7 us (2%)
    pallas_call x1, Pallas kernels, backward_call(): pl.pallas_call(functools.partial(backward_kernel, dm), out_shape=outs, in...  292 us
    pallas_call x1, Pallas kernels, forward_call(): pl.pallas_call(functools.partial(forward_kernel, dm), out_shape=outs, in_...  189 us
    psum x1, waiting for transfers between devices, reduced(): return lax.psum(parts[0], 'dp').astype(F32)  142 us
    ppermute x8, waiting for transfers between devices, reduced(): sent = lax.ppermute(parts[jnp.array(give)], 'tensor', pairs)  115 us
    psum x1, blocking collectives, shards(): small = lax.psum(small, ('tensor', 'dp'))  72.8 us
    gather x7, local copies, waits for them, and re-layouts, reduced(): parts = parts[jnp.array(keep)].astype(F32) + sent.astype(F32)  35.1 us
    gather x10, local copies, waits for them, and re-layouts, reduced(): sent = lax.ppermute(parts[jnp.array(give)], 'tensor', pairs)  25.4 us
    convert_element_type x8, other arithmetic, reduced(): parts = parts.astype(BF16)  22.4 us
  transfers between devices with their start and end apart: 9, of which 2 were waited for; matrix products, arithmetic and copies ran while one was open for 8% of the time, Pallas kernels for 0%

commit v1 on v0

--- a/solution.py
+++ b/solution.py
@@ -597,7 +597,10 @@
 
     def spread(r, _):
         rows = pl.ds(pl.multiple_of(r * STEP, STEP), STEP)
-        dyb[rows, :] = block_rows(dm, arr, rows)
+        incoming = block_rows(dm, arr, rows)
+        if T > dm.micro:
+            incoming = jnp.where(tensor < dm.micro, incoming, jnp.zeros_like(incoming))
+        dyb[rows, :] = incoming
         return 0
 
     lax.fori_loop(0, RP // STEP, spread, 0)
@@ -878,6 +881,351 @@
     )(*rest, *own, *gathered)
 
 
+def piece_list(dm):
+    down, up, out, qkv = [], [], [], []
+    for first in range(0, dm.FL, 128):
+        down.append((3, first, 128))
+    for first in range(0, dm.D, 128):
+        up.append((2, first, 128))
+    for first in range(0, dm.W, 128):
+        out.append((1, first, 128))
+    for first in range(0, 3 * dm.D, 512):
+        qkv.append((0, first, 512))
+    return down + up + out + qkv
+
+
+def reduce_kernel(
+    dm,
+    dqkv, dout, dup, ddown, flat_sums, head_sums, up_sums,
+    rqkv, rout, rup, rdown, rsmall,
+    *scratch,
+):
+    section, dp, tensor = lax.axis_index("section"), lax.axis_index("dp"), lax.axis_index("tensor")
+    T, W, D, FL, NI, C = dm.T, dm.W, dm.D, dm.FL, dm.NI, dm.C
+    line = lax.axis_size("dp")
+    stages = dm.stages
+    scratch = list(scratch)
+    mine = [scratch.pop(0) for _ in range(4)]
+    land = [[scratch.pop(0) for _ in range(4)] for _ in range(stages)]
+    inward = [scratch.pop(0) for _ in range(4)]
+    outward = [scratch.pop(0) for _ in range(4)]
+    parts, gathered, small_in, small_out, small_own = [scratch.pop(0) for _ in range(5)]
+    lsend, lrecv, isend, irecv, osend, orecv, msem, wsem, gsend, grecv, vsem = scratch
+    partial = (dqkv, dout, dup, ddown)
+    reduced = (rqkv, rout, rup, rdown)
+    pieces = piece_list(dm)
+    NP = len(pieces)
+
+    half = line // 2
+    left = dp < half
+    outer = jnp.logical_or(dp == 0, dp == line - 1)
+    middle = jnp.logical_or(dp == half - 1, dp == half)
+    toward = jnp.where(left, 1, -1)
+    inner_dp = dp + toward
+    outer_dp = lax.rem(dp - toward + line, line)
+
+    barrier = pltpu.get_barrier_semaphore()
+    for slot in range(1, T):
+        pl.semaphore_signal(barrier, inc=1, device_id={"tensor": partner(tensor, slot)})
+    pl.semaphore_signal(barrier, inc=1, device_id={"dp": lax.rem(dp + 1, line)})
+    pl.semaphore_signal(barrier, inc=1, device_id={"dp": lax.rem(dp + line - 1, line)})
+    pl.semaphore_wait(barrier, T + 1)
+
+    def at(ref, piece, *lead):
+        kind, first, rows = pieces[piece]
+        return ref[kind].at[(*lead, pl.ds(first, rows), slice(None))]
+
+    def lowest(slot):
+        stage = 0
+        while slot % 2 == 0:
+            slot //= 2
+            stage += 1
+        return stage
+
+    def fold_copy(piece, slot):
+        stage = lowest(slot)
+        bit = 1 << stage
+        source = at(partial, piece, slot) if stage == 0 else at(land[stage - 1], piece, slot >> stage)
+        return pltpu.make_async_remote_copy(
+            src_ref=source,
+            dst_ref=at(land[stage], piece, (slot - bit) >> (stage + 1)),
+            send_sem=lsend.at[piece, slot],
+            recv_sem=lrecv.at[piece, slot],
+            device_id={"tensor": flip(tensor, bit)},
+        )
+
+    def inward_copy(piece, source):
+        return pltpu.make_async_remote_copy(
+            src_ref=source,
+            dst_ref=at(inward, piece),
+            send_sem=isend.at[piece],
+            recv_sem=irecv.at[piece],
+            device_id={"dp": inner_dp},
+        )
+
+    def meet_copy(piece, source):
+        return pltpu.make_async_remote_copy(
+            src_ref=source,
+            dst_ref=at(outward, piece),
+            send_sem=isend.at[piece],
+            recv_sem=orecv.at[piece],
+            device_id={"dp": inner_dp},
+        )
+
+    def outward_copy(piece):
+        return pltpu.make_async_remote_copy(
+            src_ref=at(outward, piece),
+            dst_ref=at(outward, piece),
+            send_sem=osend.at[piece],
+            recv_sem=orecv.at[piece],
+            device_id={"dp": outer_dp},
+        )
+
+    def load(piece, slot):
+        return pltpu.make_async_copy(at(partial, piece, slot), at(mine, piece, slot // 2), msem.at[piece, slot // 2])
+
+    def store(piece):
+        return pltpu.make_async_copy(at(outward, piece), at(reduced, piece), wsem.at[piece])
+
+    for j in range(T):
+        for row in range(6):
+            parts[j, row : row + 1, :] = jnp.sum(flat_sums[row, :, j * W : (j + 1) * W], axis=0, keepdims=True)
+        parts[j, 8 + FL // W : VECTOR_ROWS, :] = jnp.zeros((VECTOR_ROWS - 8 - FL // W, W), F32)
+    per = C // W
+    for slot in range(T):
+        place = partner(tensor, slot)
+        for row in range(2):
+            parts[place, 6 + row : 7 + row, :] = jnp.sum(head_sums[slot, row], axis=0, keepdims=True)
+        for index, (owner, c) in enumerate(dm.order):
+            if owner == slot:
+                for i in range(per):
+                    row = 8 + c * per + i
+                    parts[place, row : row + 1, :] = up_sums[index, :, i * W : (i + 1) * W]
+
+    def small_copy(slot):
+        return pltpu.make_async_remote_copy(
+            src_ref=parts.at[partner(tensor, slot)],
+            dst_ref=gathered.at[slot],
+            send_sem=gsend.at[slot],
+            recv_sem=grecv.at[slot],
+            device_id={"tensor": partner(tensor, slot)},
+        )
+
+    def small_line(number, source, target, place):
+        return pltpu.make_async_remote_copy(
+            src_ref=source,
+            dst_ref=target,
+            send_sem=vsem.at[number],
+            recv_sem=vsem.at[number + 1],
+            device_id={"dp": place},
+        )
+
+    for piece in range(NP):
+        for slot in range(1, T, 2):
+            fold_copy(piece, slot).start()
+        for slot in range(0, T, 2):
+            load(piece, slot).start()
+    for slot in range(1, T):
+        small_copy(slot).start()
+
+    def rows_of(piece):
+        kind, first, rows = pieces[piece]
+        width = (W, D, FL, D)[kind]
+        step = max(16, min(rows, 32768 // width))
+        return kind, first, rows // step, step
+
+    def add_into(piece, target, sources):
+        kind, first, count, step = rows_of(piece)
+
+        def one(r, _):
+            rows = pl.ds(pl.multiple_of(first + r * step, 16), step)
+            total = target[0][kind][(*target[1], rows, slice(None))].astype(F32)
+            for ref, lead in sources:
+                total = total + ref[kind][(*lead, rows, slice(None))].astype(F32)
+            target[0][kind][(*target[1], rows, slice(None))] = total.astype(BF16)
+            return 0
+
+        lax.fori_loop(0, count, one, 0)
+
+    def pass_on(piece, stage):
+        bit = 1 << stage
+        for slot in range(bit, T, 2 * bit):
+            for before in range(stage):
+                fold_copy(piece, slot + (1 << before)).wait_recv()
+            load(piece, slot).wait()
+            add_into(
+                piece,
+                (land[stage - 1], (slot >> stage,)),
+                [(mine, (slot // 2,))] + [(land[b], (slot >> (b + 1),)) for b in range(stage - 1)],
+            )
+            fold_copy(piece, slot).start()
+
+    def own_sum(piece):
+        for stage in range(stages):
+            fold_copy(piece, 1 << stage).wait_recv()
+        load(piece, 0).wait()
+        add_into(piece, (land[stages - 1], (0,)), [(mine, (0,))] + [(land[b], (0,)) for b in range(stages - 1)])
+
+        @pl.when(outer)
+        def _():
+            inward_copy(piece, at(land[stages - 1], piece, 0)).start()
+
+    def gather_in(piece):
+        @pl.when(jnp.logical_not(outer))
+        def _():
+            inward_copy(piece, at(inward, piece)).wait_recv()
+            add_into(piece, (inward, ()), [(land[stages - 1], (0,))])
+
+            @pl.when(middle)
+            def _():
+                meet_copy(piece, at(inward, piece)).start()
+
+            @pl.when(jnp.logical_not(middle))
+            def _():
+                inward_copy(piece, at(inward, piece)).start()
+
+    def spread_middle(piece):
+        @pl.when(middle)
+        def _():
+            meet_copy(piece, at(inward, piece)).wait_recv()
+            add_into(piece, (outward, ()), [(inward, ())])
+            outward_copy(piece).start()
+            store(piece).start()
+
+    def spread_out(piece):
+        @pl.when(jnp.logical_not(middle))
+        def _():
+            outward_copy(piece).wait_recv()
+
+            @pl.when(jnp.logical_not(outer))
+            def _():
+                outward_copy(piece).start()
+
+            store(piece).start()
+
+    def small_chain():
+        for slot in range(1, T):
+            small_copy(slot).wait_recv()
+        total = parts[tensor]
+        for slot in range(1, T):
+            total = total + gathered[slot]
+        small_own[...] = total
+
+        @pl.when(outer)
+        def _():
+            small_line(0, small_own, small_in, inner_dp).start()
+
+        @pl.when(jnp.logical_not(outer))
+        def _():
+            small_line(0, small_own, small_in, inner_dp).wait_recv()
+            small_in[...] = small_in[...] + small_own[...]
+
+            @pl.when(jnp.logical_not(middle))
+            def _():
+                small_line(0, small_in, small_in, inner_dp).start()
+
+        @pl.when(middle)
+        def _():
+            meeting = small_line(2, small_in, small_out, inner_dp)
+            meeting.start()
+            meeting.wait_recv()
+            small_out[...] = small_out[...] + small_in[...]
+            small_line(4, small_out, small_out, outer_dp).start()
+
+        @pl.when(jnp.logical_not(middle))
+        def _():
+            small_line(4, small_out, small_out, outer_dp).wait_recv()
+
+            @pl.when(jnp.logical_not(outer))
+            def _():
+                small_line(4, small_out, small_out, outer_dp).start()
+
+        rsmall[...] = small_out[...]
+
+    def run(action, piece, *rest):
+        if 0 <= piece < NP:
+            action(piece, *rest)
+
+    ahead = 1
+    depth = stages - 1
+    for stage in range(1, stages):
+        for piece in range(ahead + (depth - stage)):
+            run(pass_on, piece, stage)
+    for step in range(NP + 4):
+        for stage in range(1, stages):
+            run(pass_on, step + ahead + (depth - stage), stage)
+        run(own_sum, step)
+        run(gather_in, step - 1)
+        run(spread_middle, step - 2)
+        run(spread_out, step - 3)
+        if step == NP:
+            small_chain()
+
+    for piece in range(NP):
+        store(piece).wait()
+        for slot in range(1, T):
+            fold_copy(piece, slot).wait_send()
+
+        @pl.when(jnp.logical_not(middle))
+        def _():
+            inward_copy(piece, at(inward, piece)).wait_send()
+
+        @pl.when(middle)
+        def _():
+            meet_copy(piece, at(inward, piece)).wait_send()
+
+        @pl.when(jnp.logical_not(outer))
+        def _():
+            outward_copy(piece).wait_send()
+
+    for slot in range(1, T):
+        small_copy(slot).wait_send()
+
+    @pl.when(jnp.logical_not(middle))
+    def _():
+        small_line(0, small_in, small_in, inner_dp).wait_send()
+
+    @pl.when(middle)
+    def _():
+        small_line(2, small_in, small_out, inner_dp).wait_send()
+
+    @pl.when(jnp.logical_not(outer))
+    def _():
+        small_line(4, small_out, small_out, outer_dp).wait_send()
+
+
+def reduce_call(dm, partial, sums):
+    T, W, D, FL = dm.T, dm.W, dm.D, dm.FL
+    dm.stages = T.bit_length() - 1
+    sds = jax.ShapeDtypeStruct
+    dims = ((3 * D, W), (W, D), (D, FL), (FL, D))
+    partial = (partial[0].reshape(T, 3 * D, W),) + tuple(partial[1:])
+    outs = tuple(sds(d, BF16) for d in dims) + (sds((VECTOR_ROWS, W), F32),)
+    NP = len(piece_list(dm))
+    dma = pltpu.SemaphoreType.DMA
+    scratch = [pltpu.VMEM((T // 2, *d), BF16) for d in dims]
+    for stage in range(dm.stages):
+        scratch += [pltpu.VMEM((T >> (stage + 1), *d), BF16) for d in dims]
+    scratch += [pltpu.VMEM(d, BF16) for d in dims] * 2
+    scratch += [pltpu.VMEM((T, VECTOR_ROWS, W), F32)] * 2 + [pltpu.VMEM((VECTOR_ROWS, W), F32)] * 3
+    scratch += [
+        dma((NP, T)), dma((NP, T)), dma((NP,)), dma((NP,)), dma((NP,)), dma((NP,)),
+        dma((NP, T // 2)), dma((NP,)), dma((T,)), dma((T,)), dma((6,)),
+    ]
+    whole = pl.BlockSpec(memory_space=pltpu.VMEM)
+    return pl.pallas_call(
+        functools.partial(reduce_kernel, dm),
+        out_shape=outs,
+        in_specs=[ANY] * 4 + [whole] * 3,
+        out_specs=[ANY] * 4 + [whole],
+        scratch_shapes=scratch,
+        name="grad_reduce",
+        compiler_params=pltpu.CompilerParams(
+            collective_id=2, has_side_effects=True, vmem_limit_bytes=VMEM_BYTES
+        ),
+    )(*partial, *sums)
+
+
 def shards(
     images, cotangent, ln1_gain, ln1_bias, qkv_weight, qv_bias, out_weight, out_bias,
     ln2_gain, ln2_bias, fc1_weight, fc1_bias, fc2_weight, fc2_bias,
@@ -895,40 +1243,14 @@
     dqkv, dout, dup, ddown, result, flat_sums, head_sums, up_sums = backward_call(dm, kept, own)
     input_grads = result[: dm.micro, : dm.tok][None, :, None]
 
-    def reduced(parts):
-        if T > dm.micro:
-            parts = jnp.where(tensor < dm.micro, parts, jnp.zeros_like(parts))
-        bit = 1
-        while bit < T:
-            keep = [slot for slot in range(parts.shape[0]) if slot % 2 == 0]
-            give = [slot for slot in range(parts.shape[0]) if slot % 2 == 1]
-            pairs = [(source, source ^ bit) for source in range(T)]
-            sent = lax.ppermute(parts[jnp.array(give)], "tensor", pairs)
-            parts = parts[jnp.array(keep)].astype(F32) + sent.astype(F32)
-            if parts.shape[0] > 1 or True:
-                parts = parts.astype(BF16)
-            bit *= 2
-        return lax.psum(parts[0], "dp").astype(F32)
-
-    absolute = jnp.sum(flat_sums, axis=1).reshape(6, T, W)
-    by_slot = jnp.sum(head_sums, axis=2)
-    up_rows = [None] * T
-    for index, (slot, c) in enumerate(dm.order):
-        up_rows[slot] = (up_rows[slot] or []) + [up_sums[index].reshape(-1, W)]
-    by_slot = jnp.concatenate([by_slot, jnp.stack([jnp.concatenate(rows, axis=0) for rows in up_rows])], axis=1)
-    places = jnp.stack([partner(tensor, slot) for slot in range(T)])
-    relative = jnp.zeros_like(by_slot).at[places].set(by_slot)
-    small = jnp.concatenate([absolute.transpose(1, 0, 2), relative], axis=1)
-    if T > dm.micro:
-        small = jnp.where(tensor < dm.micro, small, jnp.zeros_like(small))
-    small = lax.psum(small, ("tensor", "dp"))
-    small = lax.dynamic_index_in_dim(small, tensor, 0, keepdims=False)
+    rqkv, rout, rup, rdown, small = reduce_call(dm, (dqkv, dout, dup, ddown), (flat_sums, head_sums, up_sums))
     g2, b2, ob, db, g1, b1 = (small[i][None] for i in range(6))
     qv = small[6:8][None]
-    ub = small[8:].reshape(1, -1)
+    ub = small[8 : 8 + dm.FL // W].reshape(1, -1)
+    wide = lambda array: array.astype(F32)[None]
     return (
-        section_out, input_grads, g1, b1, reduced(dqkv)[None], qv, reduced(dout)[None], ob, g2, b2,
-        reduced(dup)[None], ub, reduced(ddown)[None], db,
+        section_out, input_grads, g1, b1, wide(rqkv.reshape(3, D, W)), qv, wide(rout), ob, g2, b2,
+        wide(rup), ub, wide(rdown), db,
     )
 
 

time: 961 us -> 693 us (0.72)
  waiting for transfers between devices: 257 us -> 0 us
  Pallas kernels: 480 us -> 654 us
  blocking collectives: 72.8 us -> 0 us
  local copies, waits for them, and re-layouts: 76.3 us -> 17.2 us
  other arithmetic: 44.7 us -> 11.8 us
  between operations: 14.7 us -> 1.15 us
    pallas_call x0 -> x1, Pallas kernels: none -> 175 us  [reduce_call(): pl.pallas_call(functools.partial(reduce_kernel, dm), out_shape=outs, in_s...]
    psum x1 -> x0, waiting for transfers between devices: 142 us -> none  [reduced(): return lax.psum(parts[0], 'dp').astype(F32)]
    ppermute x8 -> x0, waiting for transfers between devices: 115 us -> none  [reduced(): sent = lax.ppermute(parts[jnp.array(give)], 'tensor', pairs)]
    psum x1 -> x0, blocking collectives: 72.8 us -> none  [shards(): small = lax.psum(small, ('tensor', 'dp'))]
    gather x17 -> x0, local copies, waits for them, and re-layouts: 60.5 us -> none  [the longest x7 35.1 us: reduced(): parts = parts[jnp.array(keep)].astype(F32) + sent.astype(F32)]
    convert_element_type x8 -> x1, other arithmetic: 22.4 us -> 1.93 us  [shards(): wide = lambda array: array.astype(F32)[None]]
  transfers between devices with their start and end apart: 9 -> 0, of which waited for: 2 -> 0; matrix products, arithmetic and copies ran while one was open for 8% -> 0% of each run, Pallas kernels for 0% -> 0%
where the time goes in v1:
time: 693 us; the launch traced here: 684 us
  Pallas kernels  654 us (94%)
  local copies, waits for them, and re-layouts  17.2 us (2%)
  other arithmetic  11.8 us (2%)
    pallas_call x1, Pallas kernels, backward_call(): pl.pallas_call(functools.partial(backward_kernel, dm), out_shape=outs, in...  291 us
    pallas_call x1, Pallas kernels, forward_call(): pl.pallas_call(functools.partial(forward_kernel, dm), out_shape=outs, in_...  189 us
    pallas_call x1, Pallas kernels, reduce_call(): pl.pallas_call(functools.partial(reduce_kernel, dm), out_shape=outs, in_s...  175 us

profile of v1, /device:TPU:0, one launch (start us, length us, event | category | flops | bytes accessed | tf_op | source)
XLA Modules:
  0.0 684.5 jit_solution(9528831339938309080)
XLA Ops:
  0.7 0.5 broadcast.9
  1.2 1.3 reduce.3
  2.5 0.8 concatenate.3
  3.3 0.6 pad.9.spin
  4.0 1.9 fusion
  5.9 1.1 pad.8.xin
  7.0 188.8 %layer_forward.1 = (bf16[4,3,1024,256]{3,2,1,0:T(8,128)(2,1)}, bf16[4,256,1024]{2,1,0:T(8,128)(2,1)}, bf16[4,1024,1024]{2,1,0:T(8,128)(2,1)}, bf16[4,1024,1024]{...) custom-call(bf16[4,608,256]{2,1,0:T(8,128)(2,1)} %pad.8.xin, ...), custom_call_target="tpu_custom_call" | custom-call | tf_op jit(solution)/shard_map/layer_forward/pallas_call | solution.py:462
  195.8 1.4 slice_bitcast_fusion.1
  197.2 1.5 copy.30
  198.7 291.0 %layer_backward.1 = (bf16[4,3,1024,256]{3,2,1,0:T(8,128)(2,1)}, bf16[4,256,1024]{2,1,0:T(8,128)(2,1)}, bf16[4,1024,1024]{2,1,0:T(8,128)(2,1)}, bf16[4,1024,1024]...) custom-call(bf16[4,608,256]{2,1,0:T(8,128)(2,1)} %get-tuple-element., ...), custom_call_target="tpu_custom_call" | custom-call | tf_op jit(solution)/shard_map/layer_backward/pallas_call | solution.py:871
  489.6 1.8 slice_bitcast_fusion
  491.5 3.8 copy.31
  495.3 174.6 %grad_reduce.1 = (bf16[3072,256]{1,0:T(8,128)(2,1)}, bf16[256,1024]{1,0:T(8,128)(2,1)}, bf16[1024,1024]{1,0:T(8,128)(2,1)}, bf16[1024,1024]{1,0:T(8,128)(2,1)}, f32[16,256]{1,0:T(8,128)}) custom-call(bf16[4,3072,256]{2,1,0:T(8,128)(2,1)} %bitcast.35, bf16[4,256,1024]{2,1,0:T(8,128)(2,1)} %get-tuple-element.57.dout, ...), custom_call_target="tpu_custom_call" | custom-call | tf_op jit(solution)/shard_map/grad_reduce/pallas_call | solution.py:1216
  669.9 0.0 copy-start.2
  669.9 1.4 slice_bitcast_fusion.3
  671.3 0.7 slice_bitcast_fusion.2
  672.0 1.5 fusion.1
  673.5 0.6 copy.32
  674.1 2.1 bitcast_convert_fusion.2
  676.2 0.0 copy-done.2
  676.2 1.9 convert.4
  678.2 0.5 copy-done
  678.7 0.9 copy-done.1
  679.6 4.4 bitcast_convert_fusion
  (3 shorter events, 0.0 us)
Async XLA Ops:
  669.9 6.3 copy-start.2
  676.2 2.4 copy-start
  676.2 3.4 copy-start.1

commit v2 on v1

--- a/solution.py
+++ b/solution.py
@@ -43,6 +43,8 @@
     dm.FL = fc1_weight.shape[2]
     dm.RP = -(-tok // STEP) * STEP
     dm.RL = -(-tok // 128) * 128
+    dm.KR = -(-tok // 16) * 16
+    dm.HS = width // HEAD_DIM
     dm.C = min(512, dm.FL)
     dm.NC = dm.FL // dm.C
     dm.order = [
@@ -74,6 +76,15 @@
 
 def dot_plain(left, right):
     return lax.dot_general(left, right, (((1,), (0,)), ((), ())), preferred_element_type=F32)
+
+
+def add_masked(dm, scores):
+    cut = dm.tok // 8 * 8
+    if cut == dm.KR:
+        return scores
+    row = lax.broadcasted_iota(jnp.int32, (dm.KR - cut, 1), 0) + cut
+    bias = jnp.where(row < dm.tok, 0.0, MASKED).astype(F32)
+    return jnp.concatenate([scores[:cut], scores[cut:] + bias], axis=0)
 
 
 def half_masks(rows):
@@ -103,9 +114,9 @@
 def forward_kernel(
     dm,
     xin, spin, wqkv, wout, wup, wdown,
-    gqkv, gout, gup, gdown, xc, xkeep, qkeep, kkeep, vkeep, okeep, hkeep, akeep, spkeep, result,
-    xarr, n1, wq, wob, w1b, w2b, ab, gb, acc, n2, yb, b1r, spb, q, k, v, o,
-    wsend, wrecv, xsend, xrecv, psend, precv, osend, orecv, ssem, lsem, lw, la,
+    gqkv, gout, gup, gdown, xc, xkeep, qkeep, kkeep, vkeep, okeep, lkeep, hkeep, akeep, spkeep, ykeep,
+    xarr, n1, wq, wob, w1b, w2b, ab, gb, acc, n2, yb, b1r, spb, q, k, v, o, lse,
+    wsend, wrecv, xsend, xrecv, psend, precv, ssem, lsem, lw, la,
 ):
     section, tensor = lax.axis_index("section"), lax.axis_index("tensor")
     T, W, D, RP, RL, C, NI = dm.T, dm.W, dm.D, dm.RP, dm.RL, dm.C, dm.NI
@@ -141,15 +152,6 @@
             dst_ref=spb.at[tensor],
             send_sem=psend.at[slot],
             recv_sem=precv.at[slot],
-            device_id={"tensor": partner(tensor, slot)},
-        )
-
-    def output_copy(slot):
-        return pltpu.make_async_remote_copy(
-            src_ref=yb.at[partner(tensor, slot)],
-            dst_ref=result.at[tensor],
-            send_sem=osend.at[slot],
-            recv_sem=orecv.at[slot],
             device_id={"tensor": partner(tensor, slot)},
         )
 
@@ -249,9 +251,7 @@
                 arrive(slot, 0)
                 load_qkv(slot, slot % 2).start()
 
-    masks = half_masks(128)
-    lane = lax.broadcasted_iota(jnp.int32, (1, RL), 1)
-    key_bias = jnp.where(lane < dm.tok, 0.0, MASKED).astype(F32)
+    masks = half_masks(RL)
 
     fetch_qkv(0)
 
@@ -273,19 +273,20 @@
         for pair in range(W // 128):
             lanes = slice(pair * 128, pair * 128 + 128)
 
-            def block(b, _):
-                rows = pl.ds(pl.multiple_of(b * 128, 128), 128)
-                query = q[slot, rows, lanes] * jnp.asarray(HEAD_DIM**-0.5, BF16)
-                parts = []
-                for mask in masks:
-                    s = dot_last(jnp.where(mask, query, jnp.zeros_like(query)), k[slot, :, lanes]) + key_bias
-                    e = jnp.exp(s - jnp.max(s, axis=1, keepdims=True))
-                    p = (e * (1.0 / jnp.sum(e, axis=1, keepdims=True))).astype(BF16)
-                    parts.append(dot_plain(p, v[slot, :, lanes]))
-                o[slot, rows, lanes] = jnp.where(masks[0], parts[0], parts[1]).astype(BF16)
-                return 0
-
-            lax.fori_loop(0, RL // 128, block, 0, unroll=True)
+            keys, values = k[slot, pl.ds(0, dm.KR), lanes], v[slot, pl.ds(0, dm.KR), lanes]
+            query = q[slot, :, lanes] * jnp.asarray(HEAD_DIM**-0.5, BF16)
+            total = None
+            for half in range(2):
+                query_h = jnp.where(masks[half], query, jnp.zeros_like(query))
+                values_h = jnp.where(masks[half][: dm.KR], values, jnp.zeros_like(values))
+                scores = add_masked(dm, dot_last(keys, query_h))
+                most = jnp.max(scores, axis=0, keepdims=True)
+                e = jnp.exp(scores - most)
+                norm = jnp.sum(e, axis=0, keepdims=True)
+                lse[slot, pl.ds(2 * pair + half, 1), :] = most + jnp.log(norm)
+                part = dot_rows((e * (1.0 / norm)).astype(BF16), values_h)
+                total = part if total is None else total + part
+            o[slot, :, lanes] = total.astype(BF16)
 
         @pl.when(jnp.logical_and(jnp.logical_not(early), slot + 1 < T))
         def _():
@@ -296,7 +297,7 @@
     lax.fori_loop(0, T, heads, 0)
 
     keeps = []
-    for number, (source, target) in enumerate(((q, qkeep), (k, kkeep), (v, vkeep), (o, okeep))):
+    for number, (source, target) in enumerate(((q, qkeep), (k, kkeep), (v, vkeep), (o, okeep), (lse, lkeep))):
         keeps.append(pltpu.make_async_copy(source, target, la.at[2 + number]))
         keeps[-1].start()
 
@@ -370,17 +371,9 @@
         def _():
             keep_a(index - 2, parity).wait()
 
-        ab[parity] = dot_plain(n2[...], w1b[parity])
-        shift = b1r[index]
-
-        def bend(r, _):
-            rows = pl.ds(pl.multiple_of(r * STEP, STEP), STEP)
-            a = ab[parity, rows, :] + shift
-            ab[parity, rows, :] = a
-            gb[rows, :] = (0.5 * a * (1.0 + lax.erf(a * ROOT_HALF))).astype(BF16)
-            return 0
-
-        lax.fori_loop(0, RP // STEP, bend, 0)
+        a = dot_plain(n2[...], w1b[parity]) + b1r[index]
+        ab[parity] = a
+        gb[...] = (0.5 * a * (1.0 + lax.erf(a * ROOT_HALF))).astype(BF16)
         keep_a(index, parity).start()
         for n in range(D // 256):
             cols = pl.ds(n * 256, 256)
@@ -407,11 +400,9 @@
     def _():
         stream_copy.start()
 
-    for slot in range(1, T):
-        output_copy(slot).start()
-    own_out = pltpu.make_async_copy(yb.at[tensor], result.at[tensor], lsem.at[0])
-    own_out.start()
-    own_out.wait()
+    keep_y = pltpu.make_async_copy(yb, ykeep, lsem.at[0])
+    keep_y.start()
+    keep_y.wait()
     keep_x.wait()
     keep_p.wait()
     for keep in keeps:
@@ -419,7 +410,6 @@
     for index in (NI - 2, NI - 1):
         keep_a(index, index % 2).wait()
     for slot in range(1, T):
-        output_copy(slot).wait()
         vector_copy(slot).wait_send()
         input_copy(slot).wait_send()
         for index in range(dm.NCH):
@@ -446,7 +436,7 @@
         sds((T, 3, D, W), BF16), sds((T, W, D), BF16), sds((T, D, FL), BF16), sds((T, FL, D), BF16),
         sds((T, RP, W), BF16), sds((T, RP, W), BF16),
         sds((T, RL, W), BF16), sds((T, RL, W), BF16), sds((T, RL, W), BF16), sds((T, RL, W), BF16),
-        sds((RP, D), F32), sds((NI, RP, C), F32), sds((T, VECTOR_ROWS, W), F32), sds((T, RP, W), BF16),
+        sds((T, dm.HS, RL), F32), sds((RP, D), F32), sds((NI, RP, C), F32), sds((T, VECTOR_ROWS, W), F32), sds((T, RP, W), BF16),
     )
     dma = pltpu.SemaphoreType.DMA
     scratch = [
@@ -456,8 +446,9 @@
         pltpu.VMEM((RP, D), BF16), pltpu.VMEM((T, RP, W), BF16), pltpu.VMEM((NI, 1, C), F32),
         pltpu.VMEM((T, VECTOR_ROWS, W), F32),
         pltpu.VMEM((T, RL, W), BF16), pltpu.VMEM((T, RL, W), BF16), pltpu.VMEM((T, RL, W), BF16), pltpu.VMEM((T, RL, W), BF16),
-        dma((T, dm.NCH)), dma((T, dm.NCH)), dma((T,)), dma((T,)), dma((T,)), dma((T,)), dma((T,)), dma((T,)),
-        dma((2,)), dma((8,)), dma((2 + T,)), dma((6,)),
+        pltpu.VMEM((T, dm.HS, RL), F32),
+        dma((T, dm.NCH)), dma((T, dm.NCH)), dma((T,)), dma((T,)), dma((T,)), dma((T,)),
+        dma((2,)), dma((8,)), dma((2 + T,)), dma((7,)),
     ]
     return pl.pallas_call(
         functools.partial(forward_kernel, dm),
@@ -502,11 +493,11 @@
 
 def backward_kernel(
     dm,
-    xc, xkeep, qkeep, kkeep, vkeep, okeep, hkeep, akeep, spkeep,
+    xc, xkeep, qkeep, kkeep, vkeep, okeep, lkeep, hkeep, akeep, spkeep, ykeep,
     wqkv, wout, wup, wdown, gqkv, gout, gup, gdown,
-    dqkv, dout, dup, ddown, result, flat_sums, head_sums, up_sums,
+    dqkv, dout, dup, ddown, result, dxkeep, flat_sums, head_sums, up_sums,
     arr, dyb, acc, dh, hh, dhb, gs, das, n1t, n2t, nb, q, k, v, o, do, dq, dk, dv, xx,
-    w1b, w2b, ab, dgb, wob, wq, s1, s2, yb, spb, fs, hs, us, dva, dka,
+    w1b, w2b, ab, wob, wq, s1, s2, yb, spb, fs, hs, us, lse,
     ssem, osend, orecv, lsem, lw, lq, lg,
 ):
     section, tensor = lax.axis_index("section"), lax.axis_index("tensor")
@@ -530,7 +521,7 @@
 
     def output_copy(slot):
         return pltpu.make_async_remote_copy(
-            src_ref=yb.at[partner(tensor, slot)],
+            src_ref=ykeep.at[partner(tensor, slot)],
             dst_ref=result.at[tensor],
             send_sem=osend.at[slot],
             recv_sem=orecv.at[slot],
@@ -557,7 +548,7 @@
     loads = [
         pltpu.make_async_copy(source, target, lsem.at[number])
         for number, (source, target) in enumerate(
-            ((spkeep, spb), (hkeep, hh), (qkeep, q), (kkeep, k), (vkeep, v), (okeep, o), (xkeep, xx))
+            ((spkeep, spb), (hkeep, hh), (qkeep, q), (kkeep, k), (vkeep, v), (okeep, o), (xkeep, xx), (lkeep, lse))
         )
     ]
     for load in loads:
@@ -570,10 +561,14 @@
         load.start()
 
     meet(dm, section, tensor)
+    for slot in range(1, T):
+        output_copy(slot).start()
+    own_out = pltpu.make_async_copy(ykeep.at[tensor], result.at[tensor], lsem.at[8])
+    own_out.start()
 
     @pl.when(upper)
     def _():
-        load = pltpu.make_async_copy(xc, arr, lsem.at[7])
+        load = pltpu.make_async_copy(xc, arr, lsem.at[9])
         load.start()
         load.wait()
 
@@ -587,6 +582,9 @@
         das[index, tail_rows, :] = blank[:, :C]
     for slot in range(T):
         do[slot, tail_rows, :] = blank[:, :W]
+        if dm.KR < RL:
+            for ref in (dk, dv):
+                ref[slot, pl.ds(dm.KR, RL - dm.KR), :] = jnp.zeros((RL - dm.KR, W), BF16)
     acc[...] = jnp.zeros_like(acc)
     fs[...] = jnp.zeros_like(fs)
     hs[...] = jnp.zeros_like(hs)
@@ -614,19 +612,15 @@
         def _():
             fetch_ff(index + 1)
 
-        dgb[...] = dot_last(dyb[real, :], w2b[parity])
-
-        def bend(r, total):
-            rows = pl.ds(pl.multiple_of(r * STEP, STEP), STEP)
-            a = ab[parity, rows, :]
+        for first in range(0, C, 256):
+            cols = pl.ds(first, 256)
+            a = ab[parity, :, cols]
             cdf = 0.5 * (1.0 + lax.erf(a * ROOT_HALF))
-            gs[index, rows, :] = (a * cdf).astype(BF16)
-            da = dgb[rows, :] * (cdf + a * jnp.exp(-0.5 * a * a) * GAUSS_FACTOR)
-            das[index, rows, :] = da.astype(BF16)
-            return total + fold(da)
-
-        total = lax.fori_loop(0, RP // STEP, bend, jnp.zeros((8, C), F32))
-        us[index] = jnp.sum(total, axis=0, keepdims=True)
+            gs[index, real, cols] = (a * cdf).astype(BF16)
+            slope = cdf + a * jnp.exp(-0.5 * a * a) * GAUSS_FACTOR
+            da = dot_last(dyb[real, :], w2b[parity, cols, :]) * slope
+            das[index, real, cols] = da.astype(BF16)
+            us[index, :, cols] = jnp.sum(fold(da), axis=0, keepdims=True)
         for n in range(D // 256):
             cols = pl.ds(n * 256, 256)
             acc[:, cols] += dot_last(das[index, real, :], w1b[parity, cols, :])
@@ -682,10 +676,10 @@
 
             for n in range(D // 256):
                 cols = pl.ds(n * 256, 256)
-                s1[parity, cols, :] = dot_plain(n2t[cols, :], das[index]).astype(BF16)
+                s1[parity, cols, :] = dot_plain(n2t[cols, :], das[index])
             for n in range(C // 256):
                 cols = pl.ds(n * 256, 256)
-                s2[parity, cols, :] = dot_rows(gs[index, :, cols], dyb[...]).astype(BF16)
+                s2[parity, cols, :] = dot_rows(gs[index, :, cols], dyb[...])
             for j in range(NI):
 
                 @pl.when(index == j)
@@ -707,47 +701,35 @@
     for slot in range(T):
         do[slot, real, :] = dot_last(dhb[real, :], wob[pl.ds(slot * W, W), :]).astype(BF16)
 
-    mask_full = half_masks(RL)
-    row = lax.broadcasted_iota(jnp.int32, (RL, 1), 0)
-    key_bias = jnp.where(row < dm.tok, 0.0, MASKED).astype(F32)
-    scale = HEAD_DIM**-0.5
-    blocks = [(first, min(256, RL - first)) for first in range(0, RL, 256)]
+    masks = half_masks(RL)
+    scale = jnp.asarray(HEAD_DIM**-0.5, BF16)
+    real_keys = pl.ds(0, dm.KR)
 
     def heads(slot, _):
         for pair in range(W // 128):
             lanes = slice(pair * 128, pair * 128 + 128)
-            keys, values = k[slot, :, lanes], v[slot, :, lanes]
-            for number, (first, size) in enumerate(blocks):
-                rows = slice(first, first + size)
-                query, grad = q[slot, rows, lanes], do[slot, rows, lanes]
-                dq_block = jnp.zeros((size, 128), F32)
-                dk_block, dv_block = jnp.zeros((RL, 128), F32), jnp.zeros((RL, 128), F32)
-                for half in range(2):
-                    mask = mask_full[half][:size]
-                    query_h = jnp.where(mask, query, jnp.zeros_like(query))
-                    grad_h = jnp.where(mask, grad, jnp.zeros_like(grad))
-                    keys_h = jnp.where(mask_full[half], keys, jnp.zeros_like(keys))
-                    s = dot_last(keys, query_h * jnp.asarray(scale, BF16)) + key_bias
-                    e = jnp.exp(s - jnp.max(s, axis=0, keepdims=True))
-                    p = e * (1.0 / jnp.sum(e, axis=0, keepdims=True))
-                    dp = dot_last(values, grad_h)
-                    delta = jnp.sum(p * dp, axis=0, keepdims=True)
-                    ds = (p * (dp - delta) * scale).astype(BF16)
-                    dv_block = dv_block + dot_plain(p.astype(BF16), grad_h)
-                    dk_block = dk_block + dot_plain(ds, query_h)
-                    dq_block = dq_block + dot_rows(ds, keys_h)
-                dq[slot, rows, lanes] = dq_block.astype(BF16)
-                hs[slot, 0, :, lanes] += fold(dq_block)
-                if number == 0:
-                    dka[...] = dk_block
-                    dva[...] = dv_block
-                else:
-                    dka[...] += dk_block
-                    dva[...] += dv_block
-            dk[slot, :, lanes] = dka[...].astype(BF16)
-            total = dva[...]
-            dv[slot, :, lanes] = total.astype(BF16)
-            hs[slot, 1, :, lanes] += fold(total)
+            keys, values = k[slot, real_keys, lanes], v[slot, real_keys, lanes]
+            query, grad = q[slot, :, lanes] * scale, do[slot, :, lanes]
+            scaled_keys = keys * scale
+            sums = None
+            for half in range(2):
+                mask = masks[half]
+                query_h = jnp.where(mask, query, jnp.zeros_like(query))
+                grad_h = jnp.where(mask, grad, jnp.zeros_like(grad))
+                keys_h = jnp.where(mask[: dm.KR], scaled_keys, jnp.zeros_like(keys))
+                scores = add_masked(dm, dot_last(keys, query_h))
+                p = jnp.exp(scores - lse[slot, pl.ds(2 * pair + half, 1), :])
+                dp = dot_last(values, grad_h)
+                delta = jnp.sum(p * dp, axis=0, keepdims=True)
+                ds = (p * (dp - delta)).astype(BF16)
+                terms = (dot_rows(ds, keys_h), dot_plain(ds, query_h), dot_plain(p.astype(BF16), grad_h))
+                sums = terms if sums is None else tuple(x + y for x, y in zip(sums, terms))
+            dq_pair, dk_pair, dv_pair = sums
+            dq[slot, :, lanes] = dq_pair.astype(BF16)
+            dk[slot, real_keys, lanes] = dk_pair.astype(BF16)
+            dv[slot, real_keys, lanes] = dv_pair.astype(BF16)
+            hs[slot, 0, :, lanes] += fold(dq_pair)
+            hs[slot, 1, :, lanes] += fold(dv_pair)
         return 0
 
     lax.fori_loop(0, T, heads, 0)
@@ -800,32 +782,36 @@
     def _():
         down_copy.start()
 
-    for slot in range(1, T):
-        output_copy(slot).start()
-    own_out = pltpu.make_async_copy(yb.at[tensor], result.at[tensor], lsem.at[0])
-    own_out.start()
+    keep_dx = pltpu.make_async_copy(yb, dxkeep, lsem.at[0])
+    keep_dx.start()
     turn(n1t)
 
-    def put_qkv(slot, parity):
-        return [
-            pltpu.make_async_copy(s1.at[parity, :, pl.ds(0, W)], dqkv.at[slot, 0], lg.at[4 + parity]),
-            pltpu.make_async_copy(s1.at[parity, :, pl.ds(C // 2, W)], dqkv.at[slot, 1], lg.at[6 + parity]),
-        ]
-
+    pending = []
     for slot in range(T):
-        number = 0
-        s2[slot % 2, pl.ds(0, W), :] = dot_rows(o[slot], dhb[...]).astype(BF16)
-        put_out = pltpu.make_async_copy(s2.at[slot % 2, pl.ds(0, W), :], dout.at[slot], lg.at[4])
-        put_out.start()
-        for source in (dq, dk, dv):
+        for number, source in enumerate((dq, dk, dv)):
+            turn_number = len(pending) % 2
+            if len(pending) >= 2:
+                pending[-2].wait()
             for n in range(D // 256):
                 cols = pl.ds(n * 256, 256)
-                s1[number % 2, cols, pl.ds(0, W)] = dot_plain(n1t[cols, :], source[slot]).astype(BF16)
-            put = pltpu.make_async_copy(s1.at[number % 2, :, pl.ds(0, W)], dqkv.at[slot, number], lg.at[number % 2])
-            put.start()
-            put.wait()
-            number += 1
-        put_out.wait()
+                s1[turn_number, cols, pl.ds(0, W)] = dot_plain(n1t[cols, :], source[slot])
+            pending.append(
+                pltpu.make_async_copy(
+                    s1.at[turn_number, :, pl.ds(0, W)], dqkv.at[slot, number], lg.at[turn_number]
+                )
+            )
+            pending[-1].start()
+    for put in pending[-2:]:
+        put.wait()
+    pending = []
+    for slot in range(T):
+        if len(pending) >= 2:
+            pending[-2].wait()
+        s2[slot % 2, pl.ds(0, W), :] = dot_rows(o[slot], dhb[...])
+        pending.append(pltpu.make_async_copy(s2.at[slot % 2, pl.ds(0, W), :], dout.at[slot], lg.at[2 + slot % 2]))
+        pending[-1].start()
+    for put in pending[-2:]:
+        put.wait()
 
     @pl.when(upper)
     def _():
@@ -837,6 +823,7 @@
         keeps[-1].start()
     for keep in keeps:
         keep.wait()
+    keep_dx.wait()
     own_out.wait()
     for slot in range(1, T):
         output_copy(slot).wait()
@@ -849,10 +836,10 @@
 def backward_call(dm, kept, own):
     T, W, D, RP, RL, C, NI, FL = dm.T, dm.W, dm.D, dm.RP, dm.RL, dm.C, dm.NI, dm.FL
     sds = jax.ShapeDtypeStruct
-    gathered, rest = kept[:4], kept[4:13]
+    gathered, rest = kept[:4], kept[4:]
     outs = (
-        sds((T, 3, D, W), BF16), sds((T, W, D), BF16), sds((T, D, FL), BF16), sds((T, FL, D), BF16),
-        sds((T, RP, W), F32), sds((6, 8, D), F32), sds((T, 2, 8, W), F32), sds((NI, 1, C), F32),
+        sds((T, 3, D, W), F32), sds((T, W, D), F32), sds((T, D, FL), F32), sds((T, FL, D), F32),
+        sds((T, RP, W), BF16), sds((T, RP, W), F32), sds((6, 8, D), F32), sds((T, 2, 8, W), F32), sds((NI, 1, C), F32),
     )
     dma = pltpu.SemaphoreType.DMA
     heads = pltpu.VMEM((T, RL, W), BF16)
@@ -861,17 +848,17 @@
         pltpu.VMEM((RP, D), F32), pltpu.VMEM((RL, D), BF16), pltpu.VMEM((NI, RL, C), BF16), pltpu.VMEM((NI, RL, C), BF16),
         pltpu.VMEM((D, RL), BF16), pltpu.VMEM((D, RL), BF16), pltpu.VMEM((RL, D), BF16),
         heads, heads, heads, heads, heads, heads, heads, heads, pltpu.VMEM((T, RP, W), BF16),
-        pltpu.VMEM((2, D, C), BF16), pltpu.VMEM((2, C, D), BF16), pltpu.VMEM((2, RP, C), F32), pltpu.VMEM((RP, C), F32),
-        pltpu.VMEM((D, D), BF16), pltpu.VMEM((2, 3, D, W), BF16), pltpu.VMEM((2, D, C), BF16), pltpu.VMEM((2, C, D), BF16),
+        pltpu.VMEM((2, D, C), BF16), pltpu.VMEM((2, C, D), BF16), pltpu.VMEM((2, RP, C), F32),
+        pltpu.VMEM((D, D), BF16), pltpu.VMEM((2, 3, D, W), BF16), pltpu.VMEM((2, D, C), F32), pltpu.VMEM((2, C, D), F32),
         pltpu.VMEM((T, RP, W), F32), pltpu.VMEM((T, VECTOR_ROWS, W), F32),
         pltpu.VMEM((6, 8, D), F32), pltpu.VMEM((T, 2, 8, W), F32), pltpu.VMEM((NI, 1, C), F32),
-        pltpu.VMEM((RL, 128), F32), pltpu.VMEM((RL, 128), F32),
-        dma((2,)), dma((T,)), dma((T,)), dma((8,)), dma((6,)), dma((2 + T,)), dma((8,)),
+        pltpu.VMEM((T, dm.HS, RL), F32),
+        dma((2,)), dma((T,)), dma((T,)), dma((10,)), dma((6,)), dma((2 + T,)), dma((8,)),
     ]
     return pl.pallas_call(
         functools.partial(backward_kernel, dm),
         out_shape=outs,
-        in_specs=[ANY] * 17,
+        in_specs=[ANY] * 19,
         out_specs=[ANY] * len(outs),
         scratch_shapes=scratch,
         name="layer_backward",
@@ -896,8 +883,8 @@
 
 def reduce_kernel(
     dm,
-    dqkv, dout, dup, ddown, flat_sums, head_sums, up_sums,
-    rqkv, rout, rup, rdown, rsmall,
+    dqkv, dout, dup, ddown, dxkeep, flat_sums, head_sums, up_sums,
+    rqkv, rout, rup, rdown, result, fqkv, fout, fup, fdown, rsmall,
     *scratch,
 ):
     section, dp, tensor = lax.axis_index("section"), lax.axis_index("dp"), lax.axis_index("tensor")
@@ -905,12 +892,13 @@
     line = lax.axis_size("dp")
     stages = dm.stages
     scratch = list(scratch)
-    mine = [scratch.pop(0) for _ in range(4)]
+    kept, come = scratch.pop(0), scratch.pop(0)
     land = [[scratch.pop(0) for _ in range(4)] for _ in range(stages)]
     inward = [scratch.pop(0) for _ in range(4)]
     outward = [scratch.pop(0) for _ in range(4)]
     parts, gathered, small_in, small_out, small_own = [scratch.pop(0) for _ in range(5)]
-    lsend, lrecv, isend, irecv, osend, orecv, msem, wsem, gsend, grecv, vsem = scratch
+    lsend, lrecv, isend, irecv, osend, orecv, msem, wsem, gsend, grecv, vsem, dsend, drecv = scratch
+    first_land = (fqkv, fout, fup, fdown)
     partial = (dqkv, dout, dup, ddown)
     reduced = (rqkv, rout, rup, rdown)
     pieces = piece_list(dm)
@@ -945,10 +933,14 @@
     def fold_copy(piece, slot):
         stage = lowest(slot)
         bit = 1 << stage
-        source = at(partial, piece, slot) if stage == 0 else at(land[stage - 1], piece, slot >> stage)
+        place = (slot - bit) >> (stage + 1)
+        if stage == 0:
+            source, target = at(partial, piece, slot), at(first_land, piece, place)
+        else:
+            source, target = at(land[0], piece, slot // 2), at(land[stage], piece, place)
         return pltpu.make_async_remote_copy(
             src_ref=source,
-            dst_ref=at(land[stage], piece, (slot - bit) >> (stage + 1)),
+            dst_ref=target,
             send_sem=lsend.at[piece, slot],
             recv_sem=lrecv.at[piece, slot],
             device_id={"tensor": flip(tensor, bit)},
@@ -981,8 +973,30 @@
             device_id={"dp": outer_dp},
         )
 
-    def load(piece, slot):
-        return pltpu.make_async_copy(at(partial, piece, slot), at(mine, piece, slot // 2), msem.at[piece, slot // 2])
+    def loads(piece, slot):
+        kind, first, rows = pieces[piece]
+        wide = (W, D, FL, D)[kind]
+        view = (slot // 2, piece % 2, kind)
+        pair = []
+        for number, (stage, ref) in enumerate(((kept, at(partial, piece, slot)), (come, at(first_land, piece, slot // 2)))):
+            place = stage[view[2]].at[view[0], view[1]]
+            pair.append(pltpu.make_async_copy(ref, place, msem.at[number, slot // 2, piece % 2, int(kind == 0)]))
+        return pair
+
+    def fetch(piece, slot):
+        if piece < NP:
+            fold_copy(piece, slot + 1).wait_recv()
+            for one in loads(piece, slot):
+                one.start()
+
+    def input_grad_copy(slot):
+        return pltpu.make_async_remote_copy(
+            src_ref=dxkeep.at[partner(tensor, slot)],
+            dst_ref=result.at[tensor],
+            send_sem=dsend.at[slot],
+            recv_sem=drecv.at[slot],
+            device_id={"tensor": partner(tensor, slot)},
+        )
 
     def store(piece):
         return pltpu.make_async_copy(at(outward, piece), at(reduced, piece), wsem.at[piece])
@@ -1023,10 +1037,10 @@
     for piece in range(NP):
         for slot in range(1, T, 2):
             fold_copy(piece, slot).start()
-        for slot in range(0, T, 2):
-            load(piece, slot).start()
     for slot in range(1, T):
         small_copy(slot).start()
+    own_grad = pltpu.make_async_copy(dxkeep.at[tensor], result.at[tensor], dsend.at[0])
+    own_grad.start()
 
     def rows_of(piece):
         kind, first, rows = pieces[piece]
@@ -1034,14 +1048,19 @@
         step = max(16, min(rows, 32768 // width))
         return kind, first, rows // step, step
 
-    def add_into(piece, target, sources):
+    def add_into(piece, target, sources, staged=None):
         kind, first, count, step = rows_of(piece)
 
         def one(r, _):
             rows = pl.ds(pl.multiple_of(first + r * step, 16), step)
-            total = target[0][kind][(*target[1], rows, slice(None))].astype(F32)
+            near = pl.ds(pl.multiple_of(r * step, 16), step)
+            total = None
+            if staged is not None:
+                lead = (staged // 2, piece % 2, near, slice(None))
+                total = kept[kind][lead] + come[kind][lead]
             for ref, lead in sources:
-                total = total + ref[kind][(*lead, rows, slice(None))].astype(F32)
+                term = ref[kind][(*lead, rows, slice(None))].astype(F32)
+                total = term if total is None else total + term
             target[0][kind][(*target[1], rows, slice(None))] = total.astype(BF16)
             return 0
 
@@ -1050,31 +1069,40 @@
     def pass_on(piece, stage):
         bit = 1 << stage
         for slot in range(bit, T, 2 * bit):
-            for before in range(stage):
+            for before in range(1, stage):
                 fold_copy(piece, slot + (1 << before)).wait_recv()
-            load(piece, slot).wait()
+            for one in loads(piece, slot):
+                one.wait()
             add_into(
                 piece,
-                (land[stage - 1], (slot >> stage,)),
-                [(mine, (slot // 2,))] + [(land[b], (slot >> (b + 1),)) for b in range(stage - 1)],
+                (land[0], (slot // 2,)),
+                [(land[b], (slot >> (b + 1),)) for b in range(1, stage)],
+                staged=slot,
             )
             fold_copy(piece, slot).start()
+            fetch(piece + 2, slot)
+
+    own_terms = [(land[b], (0,)) for b in range(1, stages)]
 
     def own_sum(piece):
-        for stage in range(stages):
+        for stage in range(1, stages):
             fold_copy(piece, 1 << stage).wait_recv()
-        load(piece, 0).wait()
-        add_into(piece, (land[stages - 1], (0,)), [(mine, (0,))] + [(land[b], (0,)) for b in range(stages - 1)])
 
         @pl.when(outer)
         def _():
-            inward_copy(piece, at(land[stages - 1], piece, 0)).start()
+            for one in loads(piece, 0):
+                one.wait()
+            add_into(piece, (land[0], (0,)), own_terms, staged=0)
+            inward_copy(piece, at(land[0], piece, 0)).start()
+            fetch(piece + 2, 0)
 
     def gather_in(piece):
         @pl.when(jnp.logical_not(outer))
         def _():
+            for one in loads(piece, 0):
+                one.wait()
             inward_copy(piece, at(inward, piece)).wait_recv()
-            add_into(piece, (inward, ()), [(land[stages - 1], (0,))])
+            add_into(piece, (inward, ()), own_terms + [(inward, ())], staged=0)
 
             @pl.when(middle)
             def _():
@@ -1084,11 +1112,13 @@
             def _():
                 inward_copy(piece, at(inward, piece)).start()
 
+            fetch(piece + 2, 0)
+
     def spread_middle(piece):
         @pl.when(middle)
         def _():
             meet_copy(piece, at(inward, piece)).wait_recv()
-            add_into(piece, (outward, ()), [(inward, ())])
+            add_into(piece, (outward, ()), [(outward, ()), (inward, ())])
             outward_copy(piece).start()
             store(piece).start()
 
@@ -1146,6 +1176,9 @@
         if 0 <= piece < NP:
             action(piece, *rest)
 
+    for piece in range(2):
+        for slot in range(0, T, 2):
+            fetch(piece, slot)
     ahead = 1
     depth = stages - 1
     for stage in range(1, stages):
@@ -1158,6 +1191,9 @@
         run(gather_in, step - 1)
         run(spread_middle, step - 2)
         run(spread_out, step - 3)
+        if step == NP - 1:
+            for slot in range(1, T):
+                input_grad_copy(slot).start()
         if step == NP:
             small_chain()
 
@@ -1178,8 +1214,10 @@
         def _():
             outward_copy(piece).wait_send()
 
+    own_grad.wait()
     for slot in range(1, T):
         small_copy(slot).wait_send()
+        input_grad_copy(slot).wait()
 
     @pl.when(jnp.logical_not(middle))
     def _():
@@ -1194,36 +1232,38 @@
         small_line(4, small_out, small_out, outer_dp).wait_send()
 
 
-def reduce_call(dm, partial, sums):
+def reduce_call(dm, partial, dx, sums):
     T, W, D, FL = dm.T, dm.W, dm.D, dm.FL
     dm.stages = T.bit_length() - 1
     sds = jax.ShapeDtypeStruct
     dims = ((3 * D, W), (W, D), (D, FL), (FL, D))
     partial = (partial[0].reshape(T, 3 * D, W),) + tuple(partial[1:])
-    outs = tuple(sds(d, BF16) for d in dims) + (sds((VECTOR_ROWS, W), F32),)
+    outs = tuple(sds(d, BF16) for d in dims) + (sds(dx.shape, F32),)
+    outs += tuple(sds((T // 2, *d), F32) for d in dims) + (sds((VECTOR_ROWS, W), F32),)
     NP = len(piece_list(dm))
     dma = pltpu.SemaphoreType.DMA
-    scratch = [pltpu.VMEM((T // 2, *d), BF16) for d in dims]
+    staged = [pltpu.VMEM((T // 2, 2, 512, W), F32)] + [pltpu.VMEM((T // 2, 2, 128, w), F32) for w in (D, FL, D)]
+    scratch = [staged, staged]
     for stage in range(dm.stages):
-        scratch += [pltpu.VMEM((T >> (stage + 1), *d), BF16) for d in dims]
+        scratch += [pltpu.VMEM((max(T >> (stage + 1), 1), *d), BF16) for d in dims]
     scratch += [pltpu.VMEM(d, BF16) for d in dims] * 2
     scratch += [pltpu.VMEM((T, VECTOR_ROWS, W), F32)] * 2 + [pltpu.VMEM((VECTOR_ROWS, W), F32)] * 3
     scratch += [
         dma((NP, T)), dma((NP, T)), dma((NP,)), dma((NP,)), dma((NP,)), dma((NP,)),
-        dma((NP, T // 2)), dma((NP,)), dma((T,)), dma((T,)), dma((6,)),
+        dma((2, T // 2, 2, 2)), dma((NP,)), dma((T,)), dma((T,)), dma((6,)), dma((T,)), dma((T,)),
     ]
     whole = pl.BlockSpec(memory_space=pltpu.VMEM)
     return pl.pallas_call(
         functools.partial(reduce_kernel, dm),
         out_shape=outs,
-        in_specs=[ANY] * 4 + [whole] * 3,
-        out_specs=[ANY] * 4 + [whole],
+        in_specs=[ANY] * 5 + [whole] * 3,
+        out_specs=[ANY] * 9 + [whole],
         scratch_shapes=scratch,
         name="grad_reduce",
         compiler_params=pltpu.CompilerParams(
             collective_id=2, has_side_effects=True, vmem_limit_bytes=VMEM_BYTES
         ),
-    )(*partial, *sums)
+    )(*partial, dx, *sums)
 
 
 def shards(
@@ -1239,11 +1279,13 @@
     )
     own = (qkv_weight[0], out_weight[0], fc1_weight[0], fc2_weight[0])
     kept = forward_call(dm, xin, vectors, *own)
-    section_out = kept[13][: dm.micro, : dm.tok][None, :, None]
-    dqkv, dout, dup, ddown, result, flat_sums, head_sums, up_sums = backward_call(dm, kept, own)
+    dqkv, dout, dup, ddown, result, dx, flat_sums, head_sums, up_sums = backward_call(dm, kept, own)
+    section_out = result[: dm.micro, : dm.tok][None, :, None]
+
+    rqkv, rout, rup, rdown, result, _, _, _, _, small = reduce_call(
+        dm, (dqkv, dout, dup, ddown), dx, (flat_sums, head_sums, up_sums)
+    )
     input_grads = result[: dm.micro, : dm.tok][None, :, None]
-
-    rqkv, rout, rup, rdown, small = reduce_call(dm, (dqkv, dout, dup, ddown), (flat_sums, head_sums, up_sums))
     g2, b2, ob, db, g1, b1 = (small[i][None] for i in range(6))
     qv = small[6:8][None]
     ub = small[8 : 8 + dm.FL // W].reshape(1, -1)

time: 693 us -> 612 us (0.88)
  Pallas kernels: 654 us -> 584 us
    pallas_call x1, Pallas kernels: 291 us -> 217 us  [backward_call(): pl.pallas_call(functools.partial(backward_kernel, dm), out_shape=outs, in...]
where the time goes in v2:
time: 612 us; the launch traced here: 610 us
  Pallas kernels  584 us (95%)
  local copies, waits for them, and re-layouts  14.8 us (2%)
  other arithmetic  10.7 us (2%)
    pallas_call x1, Pallas kernels, backward_call(): pl.pallas_call(functools.partial(backward_kernel, dm), out_shape=outs, in...  217 us
    pallas_call x1, Pallas kernels, forward_call(): pl.pallas_call(functools.partial(forward_kernel, dm), out_shape=outs, in_...  188 us
    pallas_call x1, Pallas kernels, reduce_call(): pl.pallas_call(functools.partial(reduce_kernel, dm), out_shape=outs, in_s...  178 us

profile of v2, /device:TPU:0, one launch (start us, length us, event | category | flops | bytes accessed | tf_op | source)
XLA Modules:
  0.0 609.7 jit_solution(4131476947464782745)
XLA Ops:
  0.7 0.5 broadcast.9
  1.2 1.3 reduce.3
  2.5 0.8 concatenate.3
  3.3 0.6 pad.9.spin
  4.0 1.9 fusion
  5.9 1.1 pad.8.xin
  7.0 188.3 %layer_forward.1 = (bf16[4,3,1024,256]{3,2,1,0:T(8,128)(2,1)}, bf16[4,256,1024]{2,1,0:T(8,128)(2,1)}, bf16[4,1024,1024]{2,1,0:T(8,128)(2,1)}, bf16[4,1024,1024]{...) custom-call(bf16[4,608,256]{2,1,0:T(8,128)(2,1)} %pad.8.xin, ...), custom_call_target="tpu_custom_call" | custom-call | tf_op jit(solution)/shard_map/layer_forward/pallas_call | solution.py:453
  195.3 217.0 %layer_backward.1 = (f32[4,3,1024,256]{3,2,1,0:T(8,128)}, f32[4,256,1024]{2,1,0:T(8,128)}, f32[4,1024,1024]{2,1,0:T(8,128)}, f32[4,1024,1024]{2,1,0:T(8,128)}, b...) custom-call(bf16[4,608,256]{2,1,0:T(8,128)(2,1)} %get-tuple-element., ...), custom_call_target="tpu_custom_call" | custom-call | tf_op jit(solution)/shard_map/layer_backward/pallas_call | solution.py:858
  412.3 1.4 slice_bitcast_fusion.1
  413.7 1.5 copy.30
  415.1 178.3 %grad_reduce.1 = (bf16[3072,256]{1,0:T(8,128)(2,1)}, bf16[256,1024]{1,0:T(8,128)(2,1)}, bf16[1024,1024]{1,0:T(8,128)(2,1)}, bf16[1024,1024]{1,0:T(8,128)(2,1)}, ...) custom-call(f32[4,3072,256]{2,1,0:T(8,128)} %bitcast.29, ...), custom_call_target="tpu_custom_call" | custom-call | tf_op jit(solution)/shard_map/grad_reduce/pallas_call | solution.py:1256
  593.4 1.8 slice_bitcast_fusion
  595.2 0.0 copy-start.4
  595.3 0.0 copy-start.3
  595.3 0.0 copy-start.2
  595.3 3.8 copy.31
  599.1 0.6 slice_bitcast_fusion.3
  599.7 0.6 fusion.1
  600.3 0.6 copy.32
  600.9 1.1 bitcast_convert_fusion.2
  602.0 1.9 convert.4
  603.9 0.5 copy-done
  604.4 0.9 copy-done.1
  605.3 4.4 bitcast_convert_fusion
  (7 shorter events, 0.0 us)
Async XLA Ops:
  595.2 3.9 copy-start.4
  595.3 5.6 copy-start.3
  595.3 6.7 %copy-start.2 = (bf16[3072,256]{1,0:T(8,128)(2,1)S(1)}, bf16[3072,256]{1,0:T(8,128)(2,1)}, u32[]{:S(2)}) copy-start(bf16[3072,256]{1,0:T(8,128)(2,1)} %get-tuple-element.70) | copy-start | bytes 4718596
  602.0 2.4 copy-start
  602.0 3.4 copy-start.1

commit v3 on v2

--- a/solution.py
+++ b/solution.py
@@ -103,12 +103,16 @@
     return down.at[pl.ds(c * dm.C, dm.C), :]
 
 
-def meet(dm, section, tensor):
+def meet(dm, section, tensor, dp=None):
     barrier = pltpu.get_barrier_semaphore()
+    if dp is not None:
+        line = lax.axis_size("dp")
+        pl.semaphore_signal(barrier, inc=1, device_id={"dp": lax.rem(dp + 1, line)})
+        pl.semaphore_signal(barrier, inc=1, device_id={"dp": lax.rem(dp + line - 1, line)})
     for slot in range(1, dm.T):
         pl.semaphore_signal(barrier, inc=1, device_id={"tensor": partner(tensor, slot)})
     pl.semaphore_signal(barrier, inc=1, device_id={"section": 1 - section})
-    pl.semaphore_wait(barrier, dm.T)
+    pl.semaphore_wait(barrier, dm.T if dp is None else dm.T + 2)
 
 
 def forward_kernel(
@@ -116,9 +120,10 @@
     xin, spin, wqkv, wout, wup, wdown,
     gqkv, gout, gup, gdown, xc, xkeep, qkeep, kkeep, vkeep, okeep, lkeep, hkeep, akeep, spkeep, ykeep,
     xarr, n1, wq, wob, w1b, w2b, ab, gb, acc, n2, yb, b1r, spb, q, k, v, o, lse,
-    wsend, wrecv, xsend, xrecv, psend, precv, ssem, lsem, lw, la,
+    wsend, wrecv, xsend, xrecv, psend, precv, ssem, lsem, lw, la, fsend, hsend, frecv,
 ):
     section, tensor = lax.axis_index("section"), lax.axis_index("tensor")
+    dp, line = lax.axis_index("dp"), lax.axis_size("dp")
     T, W, D, RP, RL, C, NI = dm.T, dm.W, dm.D, dm.RP, dm.RL, dm.C, dm.NI
     lower, upper = section == 0, section == 1
     own = (wqkv, wout, wup, wdown)
@@ -155,6 +160,70 @@
             device_id={"tensor": partner(tensor, slot)},
         )
 
+    far = list(range(2, T, 2))
+    fed = dm.NCH - 2
+
+    def part_of(refs, number, origin):
+        whole = chunk_refs(dm, number + 2, *refs)
+        rows = whole.shape[0] // line
+        return whole.at[pl.ds(pl.multiple_of(origin * rows, rows), rows), :]
+
+    def far_copy(slot, number):
+        return pltpu.make_async_remote_copy(
+            src_ref=part_of(own, number, dp),
+            dst_ref=part_of(slot_refs(slot), number, dp),
+            send_sem=fsend.at[slot // 2, number],
+            recv_sem=frecv.at[slot // 2, number, dp],
+            device_id={"tensor": partner(tensor, slot)},
+        )
+
+    def hop_copy(slot, number, origin, way):
+        place = lax.rem(dp + (1 if way == 0 else line - 1), line)
+        return pltpu.make_async_remote_copy(
+            src_ref=part_of(slot_refs(slot), number, origin),
+            dst_ref=part_of(slot_refs(slot), number, origin),
+            send_sem=hsend.at[slot // 2, number, origin, way],
+            recv_sem=frecv.at[slot // 2, number, origin],
+            device_id={"dp": place},
+        )
+
+    def hop_ways(origin):
+        return (
+            jnp.logical_and(dp >= origin, dp < line - 1),
+            jnp.logical_and(dp <= origin, dp > 0),
+        )
+
+    def pass_part(slot, number, origin):
+        hop_copy(slot, number, origin, 0).wait_recv()
+        for way, go in enumerate(hop_ways(origin)):
+
+            @pl.when(go)
+            def _():
+                hop_copy(slot, number, origin, way).start()
+
+    pump_steps = fed + line - 1
+
+    def pump(step):
+        for slot in far:
+            for distance in range(line):
+                number = step - distance
+                if not 0 <= number < fed:
+                    continue
+                if distance == 0:
+                    pass_part(slot, number, dp)
+                    continue
+
+                @pl.when(dp >= distance)
+                def _():
+                    pass_part(slot, number, dp - distance)
+
+                @pl.when(dp + distance < line)
+                def _():
+                    pass_part(slot, number, dp + distance)
+
+            if 0 <= step - (line - 1) < fed:
+                weight_copy(slot + 1, step - (line - 1) + 2).start()
+
     stream_copy = pltpu.make_async_remote_copy(
         src_ref=yb,
         dst_ref=xarr,
@@ -163,7 +232,7 @@
         device_id={"section": 1 - section},
     )
 
-    meet(dm, section, tensor)
+    meet(dm, section, tensor, dp)
     for slot in range(1, T):
         vector_copy(slot).start()
         input_copy(slot).start()
@@ -171,9 +240,13 @@
     own_vec.start()
     own_in = pltpu.make_async_copy(xin.at[lax.rem(tensor, dm.micro)], xc.at[tensor], lsem.at[1])
     own_in.start()
-    direct = [slot for slot in range(1, T) if slot == 1 or slot % 2 == 0]
+    for number in range(fed):
+        for slot in far:
+            far_copy(slot, number).start()
     for index in range(dm.NCH):
-        for slot in direct:
+        weight_copy(1, index).start()
+    for index in range(2):
+        for slot in far:
             weight_copy(slot, index).start()
 
     def relay(slot, index):
@@ -188,8 +261,10 @@
 
     @pl.when(upper)
     def _():
-        for index in range(dm.NCH):
-            for slot in range(2, T, 2):
+        for step in range(pump_steps):
+            pump(step)
+        for index in range(2):
+            for slot in far:
                 relay(slot, index)
         stream_copy.wait_recv()
 
@@ -203,10 +278,11 @@
         if slot == 0:
             return
         if slot % 2 == 0:
-
-            @pl.when(lower)
-            def _():
-                relay(slot, index)
+            if index < 2:
+
+                @pl.when(lower)
+                def _():
+                    relay(slot, index)
 
         else:
             weight_copy(slot, index).wait_recv()
@@ -254,6 +330,14 @@
     masks = half_masks(RL)
 
     fetch_qkv(0)
+
+    def pump_lower(steps):
+        @pl.when(lower)
+        def _():
+            for step in steps:
+                pump(step)
+
+    pump_lower(range(1))
 
     def heads(slot, _):
         parity = lax.rem(slot, 2)
@@ -288,6 +372,15 @@
                 total = part if total is None else total + part
             o[slot, :, lanes] = total.astype(BF16)
 
+        @pl.when(jnp.logical_and(lower, slot == 0))
+        def _():
+            pump(1)
+
+        @pl.when(jnp.logical_and(lower, slot == 1))
+        def _():
+            for step in range(2, pump_steps - 2):
+                pump(step)
+
         @pl.when(jnp.logical_and(jnp.logical_not(early), slot + 1 < T))
         def _():
             fetch_qkv(slot + 1)
@@ -331,6 +424,7 @@
                     load.start()
 
     fetch_ff(0)
+    pump_lower(range(pump_steps - 2, pump_steps - 1))
     for load in loads:
         load.wait()
     attended = jnp.concatenate([o[slot, pl.ds(0, RP), :] for slot in range(T)], axis=1)
@@ -350,6 +444,7 @@
         return 0
 
     lax.fori_loop(0, RP // STEP, second_norm, 0)
+    pump_lower(range(pump_steps - 1, pump_steps))
     keep_h = pltpu.make_async_copy(acc, hkeep, lsem.at[0])
     keep_h.start()
     keep_h.wait()
@@ -412,8 +507,17 @@
     for slot in range(1, T):
         vector_copy(slot).wait_send()
         input_copy(slot).wait_send()
-        for index in range(dm.NCH):
+        for index in range(2 if slot in far else dm.NCH):
             weight_copy(slot, index).wait_send()
+    for slot in far:
+        for number in range(fed):
+            far_copy(slot, number).wait_send()
+            for origin in range(line):
+                for way, go in enumerate(hop_ways(origin)):
+
+                    @pl.when(go)
+                    def _():
+                        hop_copy(slot, number, origin, way).wait_send()
 
     @pl.when(lower)
     def _():
@@ -439,6 +543,7 @@
         sds((T, dm.HS, RL), F32), sds((RP, D), F32), sds((NI, RP, C), F32), sds((T, VECTOR_ROWS, W), F32), sds((T, RP, W), BF16),
     )
     dma = pltpu.SemaphoreType.DMA
+    line, fed = lax.axis_size("dp"), dm.NCH - 2
     scratch = [
         pltpu.VMEM((T, RP, W), BF16), pltpu.VMEM((RP, D), BF16), pltpu.VMEM((2, 3, D, W), BF16),
         pltpu.VMEM((D, D), BF16), pltpu.VMEM((2, D, C), BF16), pltpu.VMEM((2, C, D), BF16),
@@ -449,6 +554,7 @@
         pltpu.VMEM((T, dm.HS, RL), F32),
         dma((T, dm.NCH)), dma((T, dm.NCH)), dma((T,)), dma((T,)), dma((T,)), dma((T,)),
         dma((2,)), dma((8,)), dma((2 + T,)), dma((7,)),
+        dma((T // 2, fed)), dma((T // 2, fed, line, 2)), dma((T // 2, fed, line)),
     ]
     return pl.pallas_call(
         functools.partial(forward_kernel, dm),

time: 612 us -> 582 us (0.951); the launches traced: 610 us -> 573 us
  Pallas kernels: 584 us -> 546 us
    pallas_call x1, Pallas kernels: 188 us -> 148 us  [forward_call(): pl.pallas_call(functools.partial(forward_kernel, dm), out_shape=outs, in_...]
where the time goes in v3:
time: 582 us; the launch traced here: 573 us
  Pallas kernels  546 us (94%)
  local copies, waits for them, and re-layouts  14.8 us (3%)
  other arithmetic  10.7 us (2%)
    pallas_call x1, Pallas kernels, backward_call(): pl.pallas_call(functools.partial(backward_kernel, dm), out_shape=outs, in...  218 us
    pallas_call x1, Pallas kernels, reduce_call(): pl.pallas_call(functools.partial(reduce_kernel, dm), out_shape=outs, in_s...  181 us
    pallas_call x1, Pallas kernels, forward_call(): pl.pallas_call(functools.partial(forward_kernel, dm), out_shape=outs, in_...  148 us

profile of v3, /device:TPU:0, one launch (start us, length us, event | category | flops | bytes accessed | tf_op | source)
XLA Modules:
  0.0 573.0 jit_solution(4991361317227739943)
XLA Ops:
  0.7 0.5 broadcast.9
  1.2 1.3 reduce.3
  2.5 0.8 concatenate.3
  3.3 0.6 pad.9.spin
  4.0 1.9 fusion
  5.9 1.1 pad.8.xin
  7.0 148.0 %layer_forward.1 = (bf16[4,3,1024,256]{3,2,1,0:T(8,128)(2,1)}, bf16[4,256,1024]{2,1,0:T(8,128)(2,1)}, bf16[4,1024,1024]{2,1,0:T(8,128)(2,1)}, bf16[4,1024,1024]{...) custom-call(bf16[4,608,256]{2,1,0:T(8,128)(2,1)} %pad.8.xin, ...), custom_call_target="tpu_custom_call" | custom-call | tf_op jit(solution)/shard_map/layer_forward/pallas_call | solution.py:559
  155.1 217.7 %layer_backward.1 = (f32[4,3,1024,256]{3,2,1,0:T(8,128)}, f32[4,256,1024]{2,1,0:T(8,128)}, f32[4,1024,1024]{2,1,0:T(8,128)}, f32[4,1024,1024]{2,1,0:T(8,128)}, b...) custom-call(bf16[4,608,256]{2,1,0:T(8,128)(2,1)} %get-tuple-element., ...), custom_call_target="tpu_custom_call" | custom-call | tf_op jit(solution)/shard_map/layer_backward/pallas_call | solution.py:964
  372.8 1.4 slice_bitcast_fusion.1
  374.1 1.5 copy.30
  375.6 180.6 %grad_reduce.1 = (bf16[3072,256]{1,0:T(8,128)(2,1)}, bf16[256,1024]{1,0:T(8,128)(2,1)}, bf16[1024,1024]{1,0:T(8,128)(2,1)}, bf16[1024,1024]{1,0:T(8,128)(2,1)}, ...) custom-call(f32[4,3072,256]{2,1,0:T(8,128)} %bitcast.29, ...), custom_call_target="tpu_custom_call" | custom-call | tf_op jit(solution)/shard_map/grad_reduce/pallas_call | solution.py:1362
  556.2 1.8 slice_bitcast_fusion
  558.1 0.0 copy-start.4
  558.1 3.8 copy.31
  561.9 0.0 copy-done.4
  561.9 0.6 slice_bitcast_fusion.3
  562.5 0.6 fusion.1
  563.1 0.6 copy.32
  563.7 0.0 copy-done.3
  563.7 1.1 bitcast_convert_fusion.2
  564.8 1.9 convert.4
  566.7 0.5 copy-done
  567.2 0.9 copy-done.1
  568.1 4.4 bitcast_convert_fusion
  (7 shorter events, 0.0 us)
Async XLA Ops:
  558.1 3.9 copy-start.4
  558.1 5.6 copy-start.3
  558.1 6.7 %copy-start.2 = (bf16[3072,256]{1,0:T(8,128)(2,1)S(1)}, bf16[3072,256]{1,0:T(8,128)(2,1)}, u32[]{:S(2)}) copy-start(bf16[3072,256]{1,0:T(8,128)(2,1)} %get-tuple-element.70) | copy-start | bytes 4718596
  564.8 2.4 copy-start
  564.8 3.4 copy-start.1
